TPU v7x, 8 devices: a whole 2x2x1 slice. The times are simulated.
8 devices in a mesh: rep: 1 (over z), dp: 8 (over x, y, core).
Axes of the slice: x: 2, y: 2, z: 1, core: 2. Of those that a mesh axis runs over, the one named last changes fastest.
Arguments:
- x: bfloat16 [8, 2048, 1536], P(('rep', 'dp'))
- dy: bfloat16 [8, 2048, 1536], P(('rep', 'dp'))
- w_gate: bfloat16 [2, 1536, 4224], P(None, 'dp')
- w_up: bfloat16 [2, 1536, 4224], P(None, 'dp')
- w_down: bfloat16 [2, 4224, 1536], P(None, 'dp')
- m_w_gate: float32 [2, 1536, 4224], P(None, 'dp')
- m_w_up: float32 [2, 1536, 4224], P(None, 'dp')
- m_w_down: float32 [2, 4224, 1536], P(None, 'dp')
- v_w_gate: float32 [2, 1536, 4224], P(None, 'dp')
- v_w_up: float32 [2, 1536, 4224], P(None, 'dp')
- v_w_down: float32 [2, 4224, 1536], P(None, 'dp')
Outputs:
- output 1: bfloat16 [2, 1536, 4224], P('rep', 'dp')
- output 2: bfloat16 [2, 1536, 4224], P('rep', 'dp')
- output 3: bfloat16 [2, 4224, 1536], P('rep', 'dp')
- output 4: float32 [2, 1536, 4224], P('rep', 'dp')
- output 5: float32 [2, 1536, 4224], P('rep', 'dp')
- output 6: float32 [2, 4224, 1536], P('rep', 'dp')
- output 7: float32 [2, 1536, 4224], P('rep', 'dp')
- output 8: float32 [2, 1536, 4224], P('rep', 'dp')
- output 9: float32 [2, 4224, 1536], P('rep', 'dp')
All inputs are finite; a program needn't handle non-finite values.
Results may differ from a plain program's by a relative error of at most 0.022.
Values are sent between devices in bfloat16 or wider.
A program may use at most 2 GiB of HBM per device.

v0:
```python
import jax
import jax.numpy as jnp
from jax import lax
from jax.sharding import PartitionSpec as P

NAMES = ("w_gate", "w_up", "w_down")


def matmul(a, w):
    return jnp.dot(a, w, preferred_element_type=jnp.float32).astype(jnp.bfloat16)


def normed(h):
    wide = h.astype(jnp.float32)
    scale = lax.rsqrt(jnp.mean(wide**2, -1, keepdims=True) + 1e-6)
    return (wide * scale).astype(jnp.bfloat16)


def layer(h, w):
    a = normed(h)
    gate = jnp.dot(a, w["w_gate"], preferred_element_type=jnp.float32)
    up = jnp.dot(a, w["w_up"], preferred_element_type=jnp.float32)
    return h + matmul((jax.nn.silu(gate) * up).astype(jnp.bfloat16), w["w_down"])


def adamw(w, m, v, g):
    m = 0.9 * m + 0.1 * g
    v = 0.95 * v + 0.05 * g * g
    step = m * lax.rsqrt(v + 1e-8) + 0.1 * w
    return (w - 0.02 * step).astype(jnp.bfloat16), m, v


def clipped(gradients, sum_of_squares, count):
    factor = jnp.minimum(1.0, 0.5 * lax.rsqrt(sum_of_squares / count + 1e-30))
    return [g * factor for g in gradients]


def solution(mesh):
    def fetched(weights, number):
        return {name: lax.all_gather(w[number], "dp", axis=0, tiled=True) for name, w in zip(NAMES, weights, strict=True)}

    def step(x, dy, *arrays):
        weights, m, v = (arrays[i : i + 3] for i in (0, 3, 6))
        layers = weights[0].shape[0]
        h, kept = x[0], []
        for number in range(layers):
            kept.append(h)
            h = layer(h, fetched(weights, number))
        by_h, mine = dy[0], [None] * layers
        for number in reversed(range(layers)):
            _, back = jax.vjp(lambda w, h: layer(h, w), fetched(weights, number), kept[number])
            by_w, by_h = back(by_h)
            mine[number] = [lax.psum_scatter(by_w[name], "dp", scatter_dimension=0, tiled=True) for name in NAMES]
        gradients = [jnp.stack([mine[number][i] for number in range(layers)]).astype(jnp.float32) for i in range(3)]
        squares = lax.psum(sum(jnp.sum(g * g) for g in gradients), "dp")
        gradients = clipped(gradients, squares, lax.psum(1, "dp") * sum(g.size for g in gradients))
        new = [adamw(w.astype(jnp.float32), m, v, g) for w, m, v, g in zip(weights, m, v, gradients, strict=True)]
        return tuple(one[which] for which in range(3) for one in new)

    states, cut = P(("rep", "dp"), None, None), P(None, "dp", None)
    return jax.shard_map(
        step,
        mesh=mesh,
        in_specs=(states, states) + (cut,) * 9,
        out_specs=(P("rep", "dp", None),) * 9,
        check_vma=False,
    )
```

profile of v0, /device:TPU:0, one launch (start us, length us, event | category | flops | bytes accessed | tf_op | source)
XLA Modules:
  0.0 1211.0 jit_solution(17084431428621393402)
XLA Ops:
  7.2 0.0 all-gather.13.cloned.1.call-start
  7.2 4.0 fusion.102
  11.2 0.0 all-gather.13.cloned.1.call-update
  11.2 0.0 all-gather.15.cloned.1.call-start
  11.3 1.9 fusion.101
  13.2 0.0 all-gather.17.cloned.1.call-start
  13.3 3.8 fusion.100
  17.1 0.0 all-gather.17.cloned.1.call-update
  17.1 0.0 all-gather.21.cloned.1.call-start
  17.2 0.5 all-gather.21.cloned.1.call-update
  17.7 0.0 all-gather.23.cloned.1.call-start
  17.7 0.5 all-gather.23.cloned.1.call-update
  18.3 0.0 all-gather.19.cloned.1.call-start
  18.3 0.5 all-gather.19.cloned.1.call-update
  18.9 0.0 reduce-scatter.15.cloned.1.call-start
  18.9 8.6 copy.20
  27.5 4.1 fusion.34
  31.7 8.6 copy.21
  40.3 41.9 %all-gather.13.cloned.1.call-done = bf16[1,1536,4224]{2,1,0:T(8,128)(2,1)} async-done(((bf16[1,192,4224]{2,1,0:T(8,128)(2,1)}), bf16[1,1536,4224]{2,1,0:T(8,128)(2,1)}) %all-gather.13.cloned.1.call-update) | async-done | bytes 12976144 | tf_op jit(solution)/shard_map/all_gather | solution.py:40
  82.2 37.3 %fusion.32 = f32[2048,4224]{1,0:T(8,128)} fusion(bf16[1,1536,4224]{2,1,0:T(8,128)(2,1)} %all-gather.13.cloned.1.call-done, bf16[1,2048,1536]{1,2,0:T(8,128)(2,1)} %copy.20, f32[2048]{0:T(1024)S(1)} %add_rsqrt_fusion), kind=kOutput, calls=%fused_computation.51 | convolution fusion | flops 26584547328 | bytes 53878784 | tf_op jit(solution)/shard_map/dot_general | solution.py:21
  119.5 33.1 %all-gather.15.cloned.1.call-done = bf16[1,1536,4224]{2,1,0:T(8,128)(2,1)} async-done(((bf16[1,192,4224]{2,1,0:T(8,128)(2,1)}), bf16[1,1536,4224]{2,1,0:T(8,128)(2,1)}) %all-gather.15.cloned.1.call-update) | async-done | bytes 12976144 | tf_op jit(solution)/shard_map/all_gather | solution.py:40
  152.6 48.3 %multiply_convert_fusion.1 = (bf16[2048,4224]{1,0:T(8,128)(2,1)}, f32[2048,4224]{1,0:T(8,128)}) fusion(f32[2048,4224]{1,0:T(8,128)} %fusion.32, bf16[1,1536,4224]{2,1,0:T(8,128)(2,1)} %all-gather.15.cloned.1.call-done, bf16[1,2048,1536]{1,2,0:T(8,128)(2,1)} %copy.20, f32[2048]{0:T(1024)S(1)} %add_rsqrt_fusion), kind=kOutput, calls=%fused_computation.17 | convolution fusion | flops 26636451840 | bytes 105783296 | tf_op jit(solution)/shard_map/dot_general | solution.py:22
  200.9 22.0 %all-gather.17.cloned.1.call-done = bf16[1,4224,1536]{2,1,0:T(8,128)(2,1)} async-done(((bf16[1,528,1536]{2,1,0:T(8,128)(2,1)}), bf16[1,4224,1536]{2,1,0:T(8,128)(2,1)}) %all-gather.17.cloned.1.call-update) | async-done | bytes 12976144 | tf_op jit(solution)/shard_map/all_gather | solution.py:40
  223.0 48.9 %fusion.38 = (f32[2048]{0:T(1024)S(1)}, bf16[2048,1536]{0,1:T(8,128)(2,1)}) fusion(bf16[2048,4224]{1,0:T(8,128)(2,1)} %get-tuple-element.24, bf16[1,4224,1536]{2,1,0:T(8,128)(2,1)} %all-gather.17.cloned.1.call-done, bf16[1,2048,1536]{1,2,0:T(8,128)(2,1)} %copy.20), kind=kOutput, calls=%fused_computation.57 | convolution fusion | flops 26590836736 | bytes 42868736 | tf_op jit(solution)/shard_map/dot_general | solution.py:10
  271.9 0.6 copy-done.8
  272.5 20.7 %all-gather.21.cloned.1.call-done = bf16[1,4224,1536]{2,1,0:T(8,128)(2,1)} async-done(((bf16[1,528,1536]{2,1,0:T(8,128)(2,1)}), bf16[1,4224,1536]{2,1,0:T(8,128)(2,1)}) %all-gather.21.cloned.1.call-update) | async-done | bytes 12976144 | tf_op jit(solution)/shard_map/all_gather | solution.py:40
  293.2 35.7 %convolution_convert_fusion.2 = bf16[2048,4224]{1,0:T(8,128)(2,1)} fusion(bf16[1,4224,1536]{2,1,0:T(8,128)(2,1)} %all-gather.21.cloned.1.call-done, bf16[1,2048,1536]{2,1,0:T(8,128)(2,1)} %param.12), kind=kOutput, calls=%fused_computation.31 | convolution fusion | flops 26583760896 | bytes 36569088 | tf_op jit(solution)/shard_map/transpose(jvp())/dot_general | solution.py:10
  328.9 34.5 %all-gather.23.cloned.1.call-done = bf16[1,1536,4224]{2,1,0:T(8,128)(2,1)} async-done(((bf16[1,192,4224]{2,1,0:T(8,128)(2,1)}), bf16[1,1536,4224]{2,1,0:T(8,128)(2,1)}) %all-gather.23.cloned.1.call-update) | async-done | bytes 12976144 | tf_op jit(solution)/shard_map/all_gather | solution.py:40
  363.4 37.4 %fusion.19 = f32[2048,4224]{1,0:T(8,128)} fusion(bf16[1,1536,4224]{2,1,0:T(8,128)(2,1)} %all-gather.23.cloned.1.call-done, bf16[2048,1536]{0,1:T(8,128)(2,1)} %get-tuple-element.27, f32[2048]{0:T(1024)S(1)} %fusion.88), kind=kOutput, calls=%fused_computation.38 | convolution fusion | flops 26584547328 | bytes 53878784 | tf_op jit(solution)/shard_map/jvp()/dot_general | solution.py:22
  400.8 32.8 %all-gather.19.cloned.1.call-done = bf16[1,1536,4224]{2,1,0:T(8,128)(2,1)} async-done(((bf16[1,192,4224]{2,1,0:T(8,128)(2,1)}), bf16[1,1536,4224]{2,1,0:T(8,128)(2,1)}) %all-gather.19.cloned.1.call-update) | async-done | bytes 12976144 | tf_op jit(solution)/shard_map/all_gather | solution.py:40
  433.7 55.6 %fusion.2 = (bf16[2048,4224]{1,0:T(8,128)(2,1)}, f32[2048,4224]{1,0:T(8,128)}) fusion(f32[2048,4224]{1,0:T(8,128)} %fusion.19, bf16[2048,4224]{1,0:T(8,128)(2,1)} %convolution_convert_fusion.2, bf16[1,1536,4224]{2,1,0:T(8,128)(2,1)} %all-gather.19.cloned.1.call-done, bf16[2048,1536]{0,1:T(8,128)(2,1)} %get-tuple-element.27, f32[2048]{0:T(1024)S(1)} %fusion.88), kind=kOutput, calls=%fused_computation.8 | convolution fusion | flops 26688356352 | bytes 123084800 | tf_op jit(solution)/shard_map/jvp()/dot_general | solution.py:21
  489.3 36.0 %fusion.47 = bf16[2048,1536]{0,1:T(8,128)(2,1)} fusion(bf16[2048,4224]{1,0:T(8,128)(2,1)} %get-tuple-element.28, bf16[1,1536,4224]{2,1,0:T(8,128)(2,1)} %all-gather.19.cloned.1.call-done), kind=kOutput, calls=%fused_computation.79 | convolution fusion | flops 26575110144 | bytes 36569088 | tf_op jit(solution)/shard_map/transpose(jvp())/dot_general | solution.py:21
  525.3 44.8 %fusion.40 = (f32[2048]{0:T(1024)S(1)}, bf16[2048,1536]{0,1:T(8,128)(2,1)}) fusion(bf16[2048,1536]{0,1:T(8,128)(2,1)} %get-tuple-element.27, bf16[2048,1536]{0,1:T(8,128)(2,1)} %fusion.47, bf16[1,1536,4224]{2,1,0:T(8,128)(2,1)} %all-gather.23.cloned.1.call-done, bf16[2048,4224]{1,0:T(8,128)(2,1)} %convolution_convert_fusion.2, ...), kind=kOutput, calls=%fused_computation.59 | convolution fusion | flops 26645886976 | bytes 83763200 | tf_op jit(solution)/shard_map/transpose(jvp())/dot_general | solution.py:22
  570.2 8.6 fusion.71
  578.8 2.7 copy-done.4
  581.5 32.9 %convolution_convert_fusion.4 = bf16[4224,1536]{1,0:T(8,128)(2,1)} fusion(bf16[2048,4224]{1,0:T(8,128)(2,1)} %get-tuple-element.24, bf16[2048,1536]{0,1:T(8,128)(2,1)S(1)} %fusion.71), kind=kOutput, calls=%fused_computation.33 | convolution fusion | flops 26581598208 | bytes 36569088 | tf_op jit(solution)/shard_map/transpose(jvp())/dot_general | solution.py:10
  614.4 0.0 reduce-scatter.15.cloned.1.call-update
  614.4 0.0 reduce-scatter.17.cloned.1.call-start
  614.5 39.4 %convolution_convert_fusion.3 = bf16[4224,1536]{1,0:T(8,128)(2,1)} fusion(f32[2048,4224]{1,0:T(8,128)} %fusion.19, bf16[1,2048,1536]{2,1,0:T(8,128)(2,1)} %param.12, f32[2048,4224]{1,0:T(8,128)} %get-tuple-element.29), kind=kOutput, calls=%fused_computation.32 | convolution fusion | flops 26633502720 | bytes 88473600 | tf_op jit(solution)/shard_map/transpose(jvp())/dot_general | solution.py:10
  653.9 0.0 reduce-scatter.17.cloned.1.call-update
  653.9 0.0 reduce-scatter.11.cloned.1.call-start
  653.9 35.9 %convolution_convert_fusion.1 = bf16[2048,4224]{1,0:T(8,128)(2,1)} fusion(bf16[2048,1536]{0,1:T(8,128)(2,1)} %copy-done.4, bf16[1,4224,1536]{2,1,0:T(8,128)(2,1)} %all-gather.17.cloned.1.call-done), kind=kOutput, calls=%fused_computation.30 | convolution fusion | flops 26583760896 | bytes 36569088 | tf_op jit(solution)/shard_map/transpose(jvp())/dot_general | solution.py:10
  689.9 43.3 %fusion.17 = bf16[1536,4224]{1,0:T(8,128)(2,1)} fusion(bf16[2048,4224]{1,0:T(8,128)(2,1)} %convolution_convert_fusion.1, f32[2048,4224]{1,0:T(8,128)} %fusion.32, bf16[1,2048,1536]{1,2,0:T(8,128)(2,1)} %copy.20, f32[2048]{0:T(1024)S(1)} %copy-done.11), kind=kOutput, calls=%fused_computation.28 | convolution fusion | flops 26642939904 | bytes 71180288 | tf_op jit(solution)/shard_map/transpose(jvp())/dot_general | solution.py:22
  733.2 0.0 reduce-scatter.11.cloned.1.call-update
  733.2 0.0 reduce-scatter.13.cloned.1.call-start
  733.3 0.6 copy-done.7
  733.9 42.9 %fusion.13 = bf16[1536,4224]{1,0:T(8,128)(2,1)} fusion(bf16[2048,4224]{1,0:T(8,128)(2,1)} %convolution_convert_fusion.2, bf16[2048,1536]{0,1:T(8,128)(2,1)} %get-tuple-element.27, f32[2048]{0:T(1024)S(1)} %copy-done.7, f32[2048,4224]{1,0:T(8,128)} %get-tuple-element.29), kind=kOutput, calls=%fused_computation.26 | convolution fusion | flops 26642939904 | bytes 71180288 | tf_op jit(solution)/shard_map/transpose(jvp())/dot_general | solution.py:22
  776.8 0.0 reduce-scatter.13.cloned.1.call-update
  776.9 0.0 reduce-scatter.7.cloned.1.call-start
  776.9 45.6 %fusion.14 = bf16[1536,4224]{1,0:T(8,128)(2,1)} fusion(f32[2048,4224]{1,0:T(8,128)} %fusion.32, f32[2048,4224]{1,0:T(8,128)} %get-tuple-element.25, bf16[2048,4224]{1,0:T(8,128)(2,1)} %convolution_convert_fusion.1, bf16[1,2048,1536]{1,2,0:T(8,128)(2,1)} %copy.20, f32[2048]{0:T(1024)S(1)} %copy-done.11), kind=kOutput, calls=%fused_computation.27 | convolution fusion | flops 26686193664 | bytes 105783296 | tf_op jit(solution)/shard_map/transpose(jvp())/dot_general | solution.py:21
  822.5 0.0 reduce-scatter.9.cloned.1.call-start
  822.6 35.8 %convolution_convert_fusion = bf16[1536,4224]{1,0:T(8,128)(2,1)} fusion(bf16[2048,4224]{1,0:T(8,128)(2,1)} %get-tuple-element.28, bf16[2048,1536]{0,1:T(8,128)(2,1)} %get-tuple-element.27, f32[2048]{0:T(1024)S(1)} %copy-done.7), kind=kOutput, calls=%fused_computation.29 | convolution fusion | flops 26584547328 | bytes 36577280 | tf_op jit(solution)/shard_map/transpose(jvp())/dot_general | solution.py:21
  858.4 0.0 reduce-scatter.15.cloned.1.call-done
  858.4 0.0 reduce-scatter.17.cloned.1.call-done
  858.5 4.3 fusion.61
  862.8 11.6 reduce-scatter.11.cloned.1.call-done
  874.4 87.7 %reduce-scatter.13.cloned.1.call-done = bf16[192,4224]{1,0:T(8,128)(2,1)} async-done(((bf16[1536,4224]{1,0:T(8,128)(2,1)}), bf16[192,4224]{1,0:T(8,128)(2,1)}) %reduce-scatter.13.cloned.1.call-update) | async-done | bytes 1622032 | tf_op jit(solution)/shard_map/reduce_scatter | solution.py:53
  962.1 4.2 fusion.60
  966.3 83.6 %reduce-scatter.7.cloned.1.call-done = bf16[192,4224]{1,0:T(8,128)(2,1)} async-done(((bf16[1536,4224]{1,0:T(8,128)(2,1)}), bf16[192,4224]{1,0:T(8,128)(2,1)}) %reduce-scatter.7.cloned.1.call-update) | async-done | bytes 1622032 | tf_op jit(solution)/shard_map/reduce_scatter | solution.py:53
  1049.9 87.6 %reduce-scatter.9.cloned.1.call-done = bf16[192,4224]{1,0:T(8,128)(2,1)} async-done(((bf16[1536,4224]{1,0:T(8,128)(2,1)}), bf16[192,4224]{1,0:T(8,128)(2,1)}) %reduce-scatter.9.cloned.1.call-update) | async-done | bytes 1622032 | tf_op jit(solution)/shard_map/reduce_scatter | solution.py:53
  1137.5 4.2 fusion.59
  1143.6 22.6 %psum.7 = f32[]{:T(128)} all-reduce(f32[]{:T(128)S(6)} %add.99), channel_id=1, replica_groups=mesh['rep'=1,'dp'=8] {'dp'}, use_global_device_ids=true, to_apply=%region_12.13 | all-reduce | flops 1 | bytes 8 | tf_op jit(solution)/shard_map/psum | solution.py:55
  1166.9 11.9 fusion.67
  1178.8 24.8 %fusion.58 = (bf16[2,192,4224]{2,1,0:T(8,128)(2,1)}, f32[2,192,4224]{2,1,0:T(8,128)}, f32[2,192,4224]{2,1,0:T(8,128)}, bf16[2,192,4224]{2,1,0:T(8,128)(2,1)}, f3...) fusion(bf16[2,192,4224]{2,1,0:T(8,128)(2,1)S(1)} %copy-done, f32[]{:T(128)S(6)} %min_shard_map.3, ...), kind=kLoop, calls=%fused_computation.86 | loop fusion | flops 64880640 | bytes 71368704 | tf_op jit(solution)/shard_map/convert_element_type | solution.py:30
  (27 shorter events, 0.1 us)
Async XLA Ops:
  7.2 4.1 copy-start.1
  7.2 75.0 %all-gather.13.cloned.1.call-start = ((), (), s32[]{:S(2)}) async-start(), calls=%async_computation.12 | async-start | bytes 14598144 | tf_op jit(solution)/shard_map/all_gather | solution.py:40
  11.2 141.3 %all-gather.15.cloned.1.call-start = ((), (), s32[]{:S(2)}) async-start(), calls=%async_computation.13 | async-start | bytes 14598144 | tf_op jit(solution)/shard_map/all_gather | solution.py:40
  13.2 209.7 %all-gather.17.cloned.1.call-start = ((), (), s32[]{:S(2)}) async-start(), calls=%async_computation.14 | async-start | bytes 14598144 | tf_op jit(solution)/shard_map/all_gather | solution.py:40
  17.1 276.1 %all-gather.21.cloned.1.call-start = ((), (), s32[]{:S(2)}) async-start(), calls=%async_computation.16 | async-start | bytes 14598144 | tf_op jit(solution)/shard_map/all_gather | solution.py:40
  17.7 345.7 %all-gather.23.cloned.1.call-start = ((), (), s32[]{:S(2)}) async-start(), calls=%async_computation.17 | async-start | bytes 14598144 | tf_op jit(solution)/shard_map/all_gather | solution.py:40
  18.3 415.4 %all-gather.19.cloned.1.call-start = ((), (), s32[]{:S(2)}) async-start(), calls=%async_computation.15 | async-start | bytes 14598144 | tf_op jit(solution)/shard_map/all_gather | solution.py:40
  18.9 839.6 %reduce-scatter.15.cloned.1.call-start = ((), (), s32[]{:S(2)}) async-start(), calls=%async_computation.10 | async-start | bytes 14598144 | tf_op jit(solution)/shard_map/reduce_scatter | solution.py:53
  31.6 120.9 %copy-start.10 = (f32[2048]{0:T(1024)}, f32[2048]{0:T(1024)S(1)}, u32[]{:S(2)}) copy-start(f32[2048]{0:T(1024)S(1)} %add_rsqrt_fusion) | copy-start | bytes 24580
  271.9 0.6 copy-start.8
  272.5 161.2 %copy-start.5 = (f32[2048]{0:T(1024)}, f32[2048]{0:T(1024)S(1)}, u32[]{:S(2)}) copy-start(f32[2048]{0:T(1024)S(1)} %fusion.88) | copy-start | bytes 24580
  525.3 44.8 %copy-start.9 = (f32[2048]{0:T(1024)S(1)}, f32[2048]{0:T(1024)}, u32[]{:S(2)}) copy-start(f32[2048]{0:T(1024)} %copy-done.8) | copy-start | bytes 24580
  525.3 44.9 %copy-start.6 = (f32[2048]{0:T(1024)S(1)}, f32[2048]{0:T(1024)}, u32[]{:S(2)}) copy-start(f32[2048]{0:T(1024)} %copy-done.5) | copy-start | bytes 24580
  578.7 2.7 copy-start.4
  614.4 244.0 %reduce-scatter.17.cloned.1.call-start = ((), (), s32[]{:S(2)}) async-start(), calls=%async_computation.11 | async-start | bytes 14598144 | tf_op jit(solution)/shard_map/reduce_scatter | solution.py:53
  653.9 36.0 %copy-start.11 = (f32[2048]{0:T(1024)S(1)}, f32[2048]{0:T(1024)}, u32[]{:S(2)}) copy-start(f32[2048]{0:T(1024)} %copy-done.10) | copy-start | bytes 24580
  653.9 220.5 %reduce-scatter.11.cloned.1.call-start = ((), (), s32[]{:S(2)}) async-start(), calls=%async_computation.8 | async-start | bytes 14598144 | tf_op jit(solution)/shard_map/reduce_scatter | solution.py:53
  733.2 0.7 copy-start.7
  733.2 228.9 %reduce-scatter.13.cloned.1.call-start = ((), (), s32[]{:S(2)}) async-start(), calls=%async_computation.9 | async-start | bytes 14598144 | tf_op jit(solution)/shard_map/reduce_scatter | solution.py:53
  776.9 273.0 %reduce-scatter.7.cloned.1.call-start = ((), (), s32[]{:S(2)}) async-start(), calls=%async_computation.6 | async-start | bytes 14598144 | tf_op jit(solution)/shard_map/reduce_scatter | solution.py:53
  822.5 315.0 %reduce-scatter.9.cloned.1.call-start = ((), (), s32[]{:S(2)}) async-start(), calls=%async_computation.7 | async-start | bytes 14598144 | tf_op jit(solution)/shard_map/reduce_scatter | solution.py:53
  858.4 308.5 %copy-start.3 = (bf16[2,528,1536]{2,1,0:T(8,128)(2,1)S(1)}, bf16[2,528,1536]{2,1,0:T(8,128)(2,1)}, u32[]{:S(2)}) copy-start(bf16[2,528,1536]{2,1,0:T(8,128)(2,1)} %param.15) | copy-start | bytes 9732100
  1166.9 11.9 copy-start
  1166.9 11.9 copy-start.2
Sparse Core Ops, SparseCore 0:
  11.4 70.7 all-gather.12
  84.6 67.9 all-gather.14
  155.0 67.9 all-gather.16
  225.2 67.9 all-gather.20
  295.4 67.9 all-gather.22
  365.7 67.9 all-gather.18
  614.5 84.2 reduce-scatter.14
  702.3 84.2 reduce-scatter.16
  790.1 84.2 reduce-scatter.10
  877.8 84.2 reduce-scatter.12
  965.6 84.2 reduce-scatter.6
  1053.2 84.2 reduce-scatter.8
where the time goes:
time: 1220 us; the launch traced here: 1210 us
  matrix products  620 us (51%)
  waiting for transfers between devices  457 us (37%)
  other arithmetic  62.1 us (5%)
  local copies, waits for them, and re-layouts  30.9 us (3%)
  blocking collectives  22.6 us (2%)
  between operations  17.5 us (1%)
    reduce_scatter x6, waiting for transfers between devices, step(): lax.psum_scatter(by_w[name], 'dp', scatter_dimension=0, tiled=True)  271 us
    dot_general x5, matrix products, layer(): up = jnp.dot(a, w['w_up'], preferred_element_type=jnp.float32)  217 us
    dot_general x5, matrix products, layer(): gate = jnp.dot(a, w['w_gate'], preferred_element_type=jnp.float32)  210 us
    dot_general x5, matrix products, matmul(): jnp.dot(a, w, preferred_element_type=jnp.float32).astype(jnp.bfloat16)  193 us
    all_gather x6, waiting for transfers between devices, fetched(): lax.all_gather(w[number], 'dp', axis=0, tiled=True)  185 us
    convert_element_type x2, other arithmetic, adamw(): return ((w - 0.02 * step).astype(jnp.bfloat16), m, v)  36.7 us
  transfers between devices with their start and end apart: 12, of which 10 were waited for; matrix products, arithmetic and copies ran while one was open for 40% of the time, Pallas kernels for 0%

commit v1 on v0

v1 whole, which is shorter than its diff:
```python
import functools
import jax
import jax.numpy as jnp
from jax import lax
from jax.experimental import pallas as pl
from jax.experimental.pallas import tpu as pltpu
from jax.sharding import PartitionSpec as P

BF, F32 = jnp.bfloat16, jnp.float32
MESH = pl.DeviceIdType.MESH
T, D, FF = 2048, 1536, 4224
RG, RD = 192, 528
COL, WIDE, LAST = 256, 512, 128
TALL, HALF, MAIN = 1024, 768, 4096
NC = MAIN // COL
RDC, ND, PER = 176, 9, 26
Q, RING = 2 * PER, 12
DOWN, BOTH, TAIL = (RDC, WIDE), (RG, WIDE), (RG, COL)
OX, OY, OS, FX, FY, SX, SY, SD = range(8)
UNITS = ((0, (0, 8)), (0, (8, NC)), (0, None), (1, (0, 8)), (1, (8, 12)), (1, (12, NC)), (1, None))
YES, NO = True, False
S2, S3, S4 = 2, 3, 4
PAIR = (0, 1)


def cut(i, n):
    return pl.ds(i * n, n) if isinstance(i, int) else pl.ds(pl.multiple_of(i * n, n), n)


def block(i, n):
    return pl.ds(pl.multiple_of(i, 8), n)


def start(copies):
    for c in copies:
        c.start()


def wait(copies):
    for c in copies:
        c.wait()


def when(condition, do):
    if isinstance(condition, bool):
        if condition:
            do()
    else:
        pl.when(condition)(do)


def local(src, dst, sem):
    return pltpu.make_async_copy(src, dst, sem)


def dot(a, b, nt=NO):
    return lax.dot_general(a, b, (((1,), (int(nt),)), ((), ())), preferred_element_type=F32)


def gated(gate, up):
    s = jax.nn.sigmoid(gate)
    silu = gate * s
    return up * (s + silu * (1.0 - s)), silu, (silu * up).astype(BF)


def kernel(x, dy, wg, wu, wd, gg, gu, gd, squares, WG, WU, WD, aT, hT, R, Rt, h1, own, inx, iny, DG, DU,
           A, Y, dgi, d2r, sq, send, recv, keeps, dgi_sem, in_sem, out_sem, d2r_sem, d2s_sem, own_sem, sq_send, sq_recv, ld, ldl, st, credit, room):
    me = lax.axis_index("dp")
    core, y_, x_ = me % S2, (me // 2) % S2, me // 4
    at = lambda a, b, c: (a * 2 + b) * 2 + c
    xn, yn, dg, sib = at(1 - x_, y_, core), at(x_, 1 - y_, core), at(1 - x_, 1 - y_, core), at(x_, y_, 1 - core)
    other = lambda dev: dev + 1 - 2 * (dev % S2)
    everyone = [(me + k) % 8 for k in range(1, 8)]
    order = [other(dg), other(xn), other(yn), sib, dg, xn, yn, me]

    def remote(src, dst, sender, receiver, to):
        return pltpu.make_async_remote_copy(src, dst, sender, receiver, device_id={"dp": to}, device_id_type=MESH)

    def signal(sem, to):
        pl.semaphore_signal(sem, inc=1, device_id={"dp": to}, device_id_type=MESH)

    barrier = pltpu.get_barrier_semaphore()
    for dev in everyone:
        signal(barrier, dev)
    pl.semaphore_wait(barrier, len(everyone))

    to_whom = (xn, yn, sib, xn, yn, sib, sib, sib)
    whose = (me, me, me, yn, xn, xn, yn, dg)

    def half(u, p, dev):
        l, blocks = UNITS[u]
        refs = (wg, wu, wd) if dev is None else (WG, WU, WD)
        ref, height, rows, top, cols = refs[2], RD, RD // 2, p * (RD // 2), pl.ds(0, D)
        if blocks:
            lo, hi = blocks[0] * COL, FF if blocks[1] == NC else blocks[1] * COL
            ref, height, rows, top, cols = refs[p], RG, RG, 0, pl.ds(lo, hi - lo)
        if dev is not None:
            top = pl.multiple_of(dev * height + top, 8)
        return ref.at[l, pl.ds(top, rows), cols]

    def hop(u, k, p):
        src = half(u, p, None if k <= OS else whose[k])
        return remote(src, half(u, p, whose[k]), send.at[u, k, p], recv.at[u, k, p], to_whom[k])

    def keep(u):
        return [local(half(u, p, None), half(u, p, me), keeps.at[u, p]) for p in PAIR]

    def first(u):
        start(hop(u, k, p) for k, p in ((OX, 0), (OY, 1), (OX, 1), (OY, 0), (OS, 0), (OS, 1)))

    def arrived(u, *which):
        for k, p in which:
            hop(u, k, p).wait_recv()

    def point1(u):
        arrived(u, (OX, 0), (OY, 1))
        start([hop(u, FY, 0), hop(u, FX, 1)])
        if u + 1 < len(UNITS):
            first(u + 1)
        start([hop(u, SX, 0), hop(u, SY, 1)])

    def point2(u):
        arrived(u, (OX, 1), (OY, 0))
        start([hop(u, SX, 1), hop(u, SY, 0)])

    def point3(u):
        arrived(u, (FY, 0), (FX, 1))
        start(hop(u, SD, p) for p in PAIR)

    def point4(u):
        arrived(u, *((k, p) for k in (OS, SX, SY, SD) for p in PAIR))
        wait(keep(u))

    def rest(u):
        point2(u)
        point3(u)
        point4(u)

    def norm():
        @pl.loop(0, T // COL)
        def _(i):
            rows = cut(i, COL)
            wide = A[rows, :].astype(F32)
            scale = lax.rsqrt(jnp.mean(wide * wide, -1, keepdims=YES) + 1e-6)
            A[rows, :] = (wide * scale).astype(BF)

    def forward(H, hTs):
        def put_T(l, c, what):
            return local(hTs.at[c % S2], what.at[l, cut(c, COL), :], st.at[c % S2, 0])

        def transposed(l):
            n = D // COL

            @pl.loop(0, n)
            def _(c):
                pl.when(c >= 2)(lambda: put_T(l, c - 2, aT).wait())
                hTs[c % S2] = A[:, cut(c, COL)].T
                put_T(l, c, aT).start()

            wait(put_T(l, c, aT) for c in (n - 2, n - 1))

        def gate_up(u, points, Wb, r32):
            l, (lo, end) = UNITS[u]
            n = end - lo
            hi = end == NC

            def get(j):
                return [local(W.at[l, :, cut(j, COL)], Wb.at[j % S3, :, cut(i, COL)], ld.at[j % S3, i]) for i, W in enumerate((WG, WU))]

            def put(j):
                return [local(r32.at[j % S2], R.at[l, j], st.at[j % S2, 1]), put_T(l, j, hT)]

            def work(j, w, k, out):
                @pl.loop(0, 2)
                def _(i):
                    rows = cut(i, TALL)
                    r = dot(A[rows, :], Wb[k, :, pl.ds(0, 2 * w)])
                    by_gate, by_up, hid = gated(r[:, :w], r[:, w:])
                    r32[out, rows, pl.ds(0, w)] = by_gate
                    r32[out, rows, pl.ds(w, w)] = by_up
                    if l == 0:
                        H[rows, pl.ds(MAIN, w) if w == LAST else cut(j, COL)] = hid
                    hTs[out, pl.ds(0, w), rows] = hid.T

            ws = [local(W.at[l, :, pl.ds(MAIN, LAST)], Wb.at[NC % S3, :, cut(i, LAST)], ld.at[NC % S3, i]) for i, W in enumerate((WG, WU))]
            start(get(lo) + get(lo + 1))

            @pl.loop(lo, lo + n)
            def _(j):
                wait(get(j))
                pl.when(j + 2 < lo + n)(lambda: start(get(j + 2)))
                pl.when(j >= lo + 2)(lambda: wait(put(j - 2)))
                work(j, COL, j % S3, j % S2)
                start(put(j))
                if hi:
                    pl.when(j == NC - 2)(lambda: start(ws))
                for i, (do, unit) in points:
                    pl.when(j == lo + i)(lambda: do(unit))

            wait(put(lo + n - 2))
            if hi:
                wait(ws)
                work(NC, LAST, NC % S3, 0)
                outs = [local(r32.at[0, :, pl.ds(0, COL)], Rt.at[l], st.at[0, 1]), local(hTs.at[0, pl.ds(0, LAST)], hT.at[l, pl.ds(MAIN, LAST), :], st.at[0, 0])]
                start(outs)
                wait(outs)
            wait(put(lo + n - 1))

        def both(units, *points):
            def body(Wb, r32):
                for u, due in zip(units, points):
                    gate_up(u, due, Wb, r32)
                    if u < units[-1]:
                        late = [do for _, (do, unit) in due if unit == u + 1]
                        for do in (point1, point2, point3, point4):
                            if do not in late:
                                do(u + 1)

            pl.run_scoped(body, pltpu.VMEM((S3, D, WIDE), BF), pltpu.VMEM((S2, T, WIDE), F32))

        def down(Wd, xs):
            n = D // COL

            def get(c):
                return [local(WD.at[0, :, cut(c, COL)], Wd.at[c % S2], ld.at[c % S2, 0]), local(x.at[:, cut(c, COL)], xs.at[c % S2], ld.at[c % S2, 1])]

            start(get(0))

            @pl.loop(0, n)
            def _(c):
                wait(get(c))
                pl.when(c + 1 < n)(lambda: start(get(c + 1)))

                @pl.loop(0, 2)
                def _(i):
                    rows = cut(i, TALL)
                    r = dot(H[rows, :], Wd[c % S2]).astype(BF)
                    A[rows, cut(c, COL)] = (xs[c % S2, rows, :].astype(F32) + r.astype(F32)).astype(BF)

                pl.when(c == 3)(lambda: point1(3))

        load = local(x, A, ld.at[0, 0])
        load.start()
        load.wait()
        norm()
        transposed(0)
        point1(0)
        rest(0)
        both((0, 1), [(5, (point1, 1))], [(5, (point1, 2))])
        rest(2)
        pl.run_scoped(down, pltpu.VMEM((S2, FF, COL), BF), pltpu.VMEM((S2, T, COL), BF))
        save = local(A, h1, ld.at[0, 0])
        save.start()
        save.wait()
        norm()
        transposed(1)
        rest(3)
        both((3, 4, 5), [(1, (point1, 4)), (3, (point2, 4)), (5, (point3, 4))], [(0, (point1, 5)), (2, (point2, 5))], [(2, (point1, 6))])

    first(0)
    by_y = local(dy, Y, st.at[3, 0])
    by_y.start()
    for u in range(len(UNITS)):
        start(keep(u))
    pl.run_scoped(forward, pltpu.VMEM((T, FF), BF), pltpu.VMEM((S2, COL, T), BF))

    def backward(sl, pend, d2s, ow):
        def d2d(q, kind):
            r, n = kind
            rows, cols = pl.ds(0, 4 * r), pl.ds(0, n)
            return remote(d2s.at[q % S2, rows, cols], d2r.at[q % S3, rows, cols], d2s_sem.at[q % S2], d2r_sem.at[q % S3], sib)

        def halves(kind):
            r, n = kind
            return pl.ds(0, r), pl.ds(0, n // 2), pl.ds(n // 2, n // 2)

        def outs(q, kind):
            s = q % RING
            rows, lo, hi = halves(kind)
            a, b, c = sl.at[s, 0], sl.at[s, 1], sl.at[s, 2]
            ends = [(a.at[rows, lo], dgi.at[s, 0, rows, lo], dgi_sem.at[s, 0], xn), (a.at[rows, hi], dgi.at[s, 1, rows, lo], dgi_sem.at[s, 1], yn)]
            ends += [(b.at[rows, lo], inx.at[q, rows, lo], in_sem.at[q, 0], xn), (c.at[rows, hi], iny.at[q, rows, hi], in_sem.at[q, 1], yn)]
            ends += [(b.at[rows, hi], inx.at[q, rows, hi], in_sem.at[q, 2], xn), (c.at[rows, lo], iny.at[q, rows, lo], in_sem.at[q, 3], yn)]
            return [remote(src, dst, out_sem.at[s, i], sem, to) for i, (src, dst, sem, to) in enumerate(ends)]

        def by_kind(q, do):
            c = q % PER
            pl.when(c < ND)(lambda: do(q, DOWN))
            pl.when(jnp.logical_and(c >= ND, c < PER - 1))(lambda: do(q, BOTH))
            pl.when(c == PER - 1)(lambda: do(q, TAIL))

        def release(q, kind):
            for c in outs(q, kind):
                c.wait_send()

        def put_own(q, kind):
            r, n = kind
            return local(ow.at[q % S2, pl.ds(0, r), pl.ds(0, n)], own.at[q, pl.ds(0, r), pl.ds(0, n)], own_sem.at[q % S2])

        def wait_own(q, kind):
            put_own(q, kind).wait()

        def before_add(q, kind):
            when(q >= RING, lambda: by_kind(jnp.int32(q - RING), release))
            c = d2d(q, kind)
            c.wait_recv()
            c.wait_send()
            when(q >= 2, lambda: by_kind(jnp.int32(q - 2), wait_own))

        def sums(q, kind, lhs, rhs):
            r, n = kind
            h, s = n // 2, q % RING
            rows, lo, hi = halves(kind)
            t = dot(lhs[pl.ds(4 * r, 4 * r), :], rhs) + d2r[q % S3, pl.ds(0, 4 * r), pl.ds(0, n)].astype(F32)
            sl[s, 0, rows, pl.ds(0, n)] = t[:r].astype(BF)
            sl[s, 1, rows, lo] = t[r : 2 * r, :h].astype(BF)
            pend[s, 1, rows, lo] = t[r : 2 * r, h:]
            sl[s, 2, rows, hi] = t[2 * r : 3 * r, h:].astype(BF)
            pend[s, 0, rows, lo] = t[2 * r : 3 * r, :h]
            ow[q % S2, rows, pl.ds(0, n)] = t[3 * r :]

        def theirs(q, kind, lhs, rhs):
            r, n = kind
            d2s[q % S2, pl.ds(0, 4 * r), pl.ds(0, n)] = dot(lhs[pl.ds(0, 4 * r), :], rhs).astype(BF)

        def after_add(q, kind):
            def room_there():
                for i in PAIR:
                    pl.semaphore_wait(room.at[i], 1)

            when(q >= RING, room_there)
            start(outs(q, kind)[:4])
            put_own(q, kind).start()
            when(q < Q - 3, lambda: signal(credit, sib))

        def send_d2d(q, kind):
            when(q >= 3, lambda: pl.semaphore_wait(credit, 1))
            d2d(q, kind).start()

        def serve(q, kind):
            s = q % RING
            rows, lo, hi = halves(kind)
            o = outs(q, kind)
            for c in o[:2]:
                c.wait_recv()
            sl[s, 2, rows, lo] = (pend[s, 0, rows, lo] + dgi[s, 0, rows, lo].astype(F32)).astype(BF)
            sl[s, 1, rows, hi] = (pend[s, 1, rows, lo] + dgi[s, 1, rows, lo].astype(F32)).astype(BF)
            start(o[4:])

            def done():
                for i, dev in enumerate((xn, yn)):
                    signal(room.at[i], dev)

            when(q < Q - RING, done)

        def serve_some(i, steps, lo, count, kind):
            a, b = (i * count) // steps, ((i + 1) * count) // steps
            pl.when(jnp.logical_and(b > a, jnp.logical_and(i >= 0, i < steps)))(lambda: serve(lo + a, kind))

        def down_gradient(base, l, then):
            def body(L):
                def get(t):
                    return [local(hT.at[l, block(dev * RD + t * RDC, RDC), :], L.at[t % S2, cut(b, RDC), :], ldl.at[t % S2, b]) for b, dev in enumerate(order)]

                def one(c, do_s, do_m):
                    q, e = base + c, c - 2
                    if do_s:
                        pl.when(c % S3 == 0)(lambda: wait(get(c // 3)))
                        pl.when(jnp.logical_and(c % S3 == 2, c < ND - 1))(lambda: start(get(c // 3 + 1)))
                    if do_m:
                        before_add(q - 2, DOWN)
                        sums(q - 2, DOWN, L.at[(e // 3) % S2], Y[:, cut(e % S3, WIDE)])
                    if do_s:
                        theirs(q, DOWN, L.at[(c // 3) % S2], Y[:, cut(c % S3, WIDE)])
                        send_d2d(q, DOWN)
                    if do_m:
                        after_add(q - 2, DOWN)

                start(get(0))
                @pl.loop(0, 2)
                def _(c):
                    one(c, YES, NO)

                @pl.loop(2, ND)
                def _(c):
                    one(c, YES, YES)
                    if l == 1:
                        pl.when(c == 2)(lambda: point2(6))
                        pl.when(c == 7)(lambda: point3(6))
                    else:
                        serve_some(c - 5, S4, base, S3, DOWN)

                then()

                @pl.loop(ND, ND + 2)
                def _(c):
                    one(c, NO, YES)

            pl.run_scoped(body, pltpu.VMEM((S2, 8 * RDC, T), BF))

        def layer_gradients(base, l):
            g = base + ND

            def outer(Wd, Rb, dgu):
                lhs = lambda L: [local(aT.at[l, block(dev * RG, RG), :], L.at[cut(b, RG), :], ldl.at[2, b]) for b, dev in enumerate(order)]
                is_last = lambda c: isinstance(c, int) and c == NC
                kind = lambda c: TAIL if is_last(c) else BOTH
                part = lambda c: dgu[c % S4, :, pl.ds(0, kind(c)[1])]

                def get(c):
                    k = c % S2
                    if is_last(c):
                        return [local(WD.at[l, pl.ds(MAIN, LAST), :], Wd.at[k, pl.ds(0, LAST), :], ld.at[k, 0]), local(Rt.at[l], Rb.at[k, :, pl.ds(0, COL)], ld.at[k, 1])]
                    return [local(WD.at[l, cut(c, COL), :], Wd.at[k], ld.at[k, 0]), local(R.at[l, c], Rb.at[k], ld.at[k, 1])]

                def put(c):
                    w, cols = (LAST, pl.ds(MAIN, LAST)) if is_last(c) else (COL, cut(c, COL))
                    return [local(dgu.at[c % S4, :, cut(i, w)], W.at[:, cols], st.at[c % S4, i]) for i, W in enumerate((DG, DU))]

                def step(s, L, do_f, do_s, do_m):
                    c, e = s - 1, s - 3
                    if do_f:
                        wait(get(s))
                        when(jnp.logical_and(s > 0, s < NC - 1) if not isinstance(s, int) else 0 < s < NC - 1, lambda: start(get(s + 1)))
                        if l == 1:
                            when(s >= 4, lambda: wait(put(s - 4)))
                    if do_m:
                        before_add(g + e, kind(e))
                        sums(g + e, kind(e), L, part(e))
                    if do_s:
                        theirs(g + c, kind(c), L, part(c))
                    if do_f:
                        w = LAST if is_last(s) else COL
                        d = dot(Y[...], Wd[s % S2, pl.ds(0, w), :], nt=YES).astype(BF).astype(F32)
                        for i in PAIR:
                            dgu[s % S4, :, cut(i, w)] = (d * Rb[s % S2, :, cut(i, w)]).astype(BF)
                    if do_s:
                        send_d2d(g + c, kind(c))
                    if do_f and l == 1:
                        start(put(s))
                    if do_m:
                        after_add(g + e, kind(e))

                def down_served(s):
                    if l == 1:
                        serve_some(2 * s, 12, base, ND, DOWN)
                        serve_some(2 * s + 1, 12, base, ND, DOWN)
                    else:
                        serve_some(s, ND - S3, base + S3, ND - S3, DOWN)

                def ahead():
                    if l == 1:
                        point4(6)
                    start(get(0) + get(1))

                def body(L):
                    start(lhs(L))
                    step(0, L, YES, NO, NO)
                    down_served(jnp.int32(0))
                    wait(lhs(L))

                    @pl.loop(1, 3)
                    def _(s):
                        step(s, L, YES, YES, NO)
                        down_served(s)

                    @pl.loop(3, NC)
                    def _(s):
                        step(s, L, YES, YES, YES)
                        pl.when(s == NC - 2)(lambda: start(get(NC)))
                        down_served(s)
                        serve_some(s - 6, 11, g, 10, BOTH)

                    step(NC, L, YES, YES, YES)
                    serve(g + 9, BOTH)
                    step(NC + 1, L, NO, YES, YES)
                    step(NC + 2, L, NO, NO, YES)
                    step(NC + 3, L, NO, NO, YES)
                    if l == 1:
                        for c in range(NC - 3, NC + 1):
                            wait(put(c))

                down_gradient(base, l, ahead)
                pl.run_scoped(body, pltpu.VMEM((D, T), BF))

            V = pltpu.VMEM
            pl.run_scoped(outer, V((S2, COL, D), BF), V((S2, T, WIDE), F32), V((S4, T, WIDE), BF))

        def input_gradient():
            m, n = T // WIDE, D // HALF
            steps = m * n

            def body(W, X, hb):
                def get_x(i, src):
                    return [local(src.at[cut(i % m * 4 + k, LAST), :], X.at[i % S2, cut(k, LAST), :], ldl.at[i % S2, k]) for k in range(4)]

                def get_w(k, src):
                    return local(src.at[1, cut(k % n, HALF), :], W.at[k % S2], ld.at[k % S2, 1])

                get_w(0, WG).start()
                start(get_x(0, DG))
                for up, (grad, weight) in enumerate(((DG, WG), (DU, WU))):
                    @pl.loop(0, steps)
                    def _(i):
                        k = n * up + i // m

                        @pl.when(i % m == 0)
                        def _():
                            get_w(k, weight).wait()
                            pl.when(i < steps - m)(lambda: get_w(k + 1, weight).start())
                            if not up:
                                pl.when(i == steps - m)(lambda: get_w(n, WU).start())

                        wait(get_x(i, grad))
                        pl.when(i < steps - 1)(lambda: start(get_x(i + 1, grad)))
                        if not up:
                            pl.when(i == steps - 1)(lambda: start(get_x(0, DU)))
                        r = dot(X[i % S2], W[k % S2], nt=YES).astype(BF)
                        place = (cut(i % m, WIDE), cut(i // m, HALF))
                        A[place] = (A[place].astype(F32) + r.astype(F32)).astype(BF) if up else r
                        serve_some(steps * up + i, 11, ND + 10, 6, BOTH)

                get_h = lambda i: local(h1.at[cut(i, COL), :], hb.at[i % S2], st.at[i % S2, 0])
                get_h(0).start()
                serve(PER - 1, TAIL)

                @pl.loop(0, T // COL)
                def _(i):
                    get_h(i).wait()
                    pl.when(i < T // COL - 1)(lambda: get_h(i + 1).start())
                    rows = cut(i, COL)
                    f, b = hb[i % S2].astype(F32), A[rows, :].astype(F32)
                    ms = jnp.mean(f * f, -1, keepdims=YES) + 1e-6
                    scale = lax.rsqrt(ms)
                    c = jnp.sum(f * b, -1, keepdims=YES) * (-0.5 * (scale / ms)) * (1.0 / D)
                    back = (b * scale + c * (2.0 * f)).astype(BF)
                    Y[rows, :] = (Y[rows, :].astype(F32) + back.astype(F32)).astype(BF)

            V = pltpu.VMEM
            pl.run_scoped(body, V((S2, HALF, FF), BF), V((S2, WIDE, FF), BF), V((S2, COL, D), BF))

        by_y.wait()
        layer_gradients(0, 1)
        input_gradient()
        layer_gradients(PER, 0)

        for q in (Q - 2, Q - 1):
            by_kind(jnp.int32(q), wait_own)

        def finish(ob, ib, gb, acc):
            def get(q):
                return [local(own.at[q], ob.at[q % S3], ldl.at[q % S3, 0])] + [local(src.at[q], ib.at[q % S3, i], ldl.at[q % S3, i + 1]) for i, src in enumerate((inx, iny))]

            def fetch(q):
                def all_in(q, kind):
                    for c in outs(q, kind)[2:]:
                        c.wait_recv()

                by_kind(q, all_in)
                start(get(q))

            def put(q, kind):
                l, c, s = 1 - q // PER, q % PER, q % S2
                if kind == DOWN:
                    return [local(gb.at[s, pl.ds(0, RDC), :], gd.at[l, cut(c // 3, RDC), cut(c % S3, WIDE)], st.at[s, 0])]
                w = LAST if kind == TAIL else COL
                cols = pl.ds(MAIN, LAST) if kind == TAIL else cut(c - ND, COL)
                return [local(gb.at[s, :, cut(i, w)], dst.at[l, :, cols], st.at[s, i]) for i, dst in enumerate((gg, gu))]

            def one(q):
                pl.when(q < Q - 2)(lambda: fetch(q + 2))
                pl.when(q >= 2)(lambda: by_kind(q - 2, lambda q, kind: wait(put(q, kind))))
                wait(get(q))
                c, s = q % PER, q % S3
                height, width = jnp.where(c < ND, RDC, RG), jnp.where(c == PER - 1, COL, WIDE)
                inside = jnp.logical_and(lax.broadcasted_iota(jnp.int32, (RG, WIDE), 0) < height, lax.broadcasted_iota(jnp.int32, (RG, WIDE), 1) < width)
                g = (ob[s] + ib[s, 0].astype(F32) + ib[s, 1].astype(F32)).astype(BF)
                gb[q % S2] = g
                g = jnp.where(inside, g.astype(F32), 0.0)
                acc[...] += jnp.sum((g * g).reshape(RG // 8, 8, WIDE), 0)
                by_kind(q, lambda q, kind: start(put(q, kind)))

            acc[...] = jnp.zeros_like(acc)
            n = 7
            left = Q - n
            fetch(jnp.int32(0))
            fetch(jnp.int32(1))

            @pl.loop(0, n * (Q - left))
            def _(q):
                pl.when(q % n == 0)(lambda: by_kind(left + q // n, serve))
                one(q)

            @pl.loop(n * (Q - left), Q)
            def _(q):
                one(q)

            for q in (Q - 2, Q - 1):
                by_kind(jnp.int32(q), lambda q, kind: wait(put(q, kind)))
            sq[me] = sum(acc[:, cut(i, LAST)] for i in range(WIDE // LAST))

        V = pltpu.VMEM
        pl.run_scoped(finish, V((S3, RG, WIDE), F32), V((S3, 2, RG, WIDE), BF), V((S2, RG, WIDE), BF), V((8, WIDE), F32))
        tell = [remote(sq.at[me], sq.at[me], sq_send.at[k], sq_recv.at[k], dev) for k, dev in enumerate(everyone)]
        start(tell)
        @pl.loop(Q - RING, Q)
        def _(q):
            by_kind(q, release)

        for u in range(len(UNITS)):
            for k in range(8):
                for p in ((1,) if k == FX else (0,) if k == FY else (0, 1)):
                    hop(u, k, p).wait_send()
        wait(tell)
        sq[0] = sum(sq[i] for i in range(8))
        out = local(sq.at[0], squares, ld.at[0, 0])
        out.start()
        out.wait()

    V = pltpu.VMEM
    pl.run_scoped(backward, V((RING, 3, RG, WIDE), BF), V((RING, 2, RG, COL), F32), V((S2, 4 * RG, WIDE), BF), V((S2, RG, WIDE), F32))


def gradients_of(x, dy, wg, wu, wd):
    S, V = jax.ShapeDtypeStruct, pltpu.VMEM
    dma, regular = pltpu.SemaphoreType.DMA, pltpu.SemaphoreType.REGULAR
    anywhere = pl.BlockSpec(memory_space=pl.ANY)
    narrow, wide = [
        [(2, RG, FF), (2, RG, FF), (2, RD, D)],
        [(8, LAST)],
    ]
    outs = [S(s, BF) for s in narrow] + [S(s, F32) for s in wide]
    outs += [S((S2, D, FF), BF), S((S2, D, FF), BF), S((S2, FF, D), BF), S((S2, D, T), BF), S((S2, FF, T), BF), S((S2, NC, T, WIDE), F32), S((S2, T, COL), F32), S((T, D), BF)]
    outs += [S((Q, RG, WIDE), F32), S((Q, RG, WIDE), BF), S((Q, RG, WIDE), BF), S((T, FF), BF), S((T, FF), BF)]
    scratch = [V((T, D), BF), V((T, D), BF), V((RING, 2, RG, COL), BF), V((S3, 4 * RG, WIDE), BF), V((8, 8, LAST), F32)]
    scratch += [dma((len(UNITS), 8, 2)), dma((len(UNITS), 8, 2)), dma((len(UNITS), 2)), dma((RING, 2)), dma((Q, 4)), dma((RING, 6)), dma((3,)), dma((2,)), dma((2,)), dma((7,)), dma((7,))]
    scratch += [dma((3, 2)), dma((3, 8)), dma((4, 2)), regular, regular((2,))]
    return pl.pallas_call(
        kernel,
        out_shape=outs,
        in_specs=[anywhere] * 5,
        out_specs=[anywhere] * len(outs),
        scratch_shapes=scratch,
        compiler_params=pltpu.CompilerParams(collective_id=0, has_side_effects=YES, vmem_limit_bytes=67_000_000),
        name="step",
    )(x, dy, wg, wu, wd)[:4]


def adamw(w, m, v, g):
    m = 0.9 * m + 0.1 * g
    v = 0.95 * v + 0.05 * g * g
    step = m * lax.rsqrt(v + 1e-8) + 0.1 * w
    return (w - 0.02 * step).astype(BF), m, v


def solution(mesh):
    def step(x, dy, *arrays):
        weights, m, v = (arrays[i : i + 3] for i in (0, 3, 6))
        *gradients, squares = gradients_of(x[0], dy[0], *weights)
        count = mesh.shape["dp"] * sum(g.size for g in gradients)
        factor = jnp.minimum(1.0, 0.5 * lax.rsqrt(jnp.sum(squares) / count + 1e-30))
        new = [adamw(w.astype(F32), m, v, g.astype(F32) * factor) for w, m, v, g in zip(weights, m, v, gradients, strict=YES)]
        return tuple(one[which] for which in range(3) for one in new)

    states, cuts = P(("rep", "dp"), None, None), P(None, "dp", None)
    return jax.shard_map(
        step,
        mesh=mesh,
        in_specs=(states, states) + (cuts,) * 9,
        out_specs=(P("rep", "dp", None),) * 9,
        check_vma=NO,
    )
```

time: 1220 us -> 735 us (0.60)
  Pallas kernels: 0 us -> 685 us
  matrix products: 620 us -> 0 us
  waiting for transfers between devices: 457 us -> 0 us
  local copies, waits for them, and re-layouts: 30.9 us -> 1.17 us
  other arithmetic: 62.1 us -> 38.8 us
  blocking collectives: 22.6 us -> 0 us
  between operations: 17.5 us -> 1.81 us
    pallas_call x0 -> x1, Pallas kernels: none -> 685 us  [gradients_of(): pl.pallas_call(kernel, out_shape=outs, in_specs=[anywhere] * 5, out_specs...]
    dot_general x15 -> x0, matrix products: 620 us -> none  [the longest x5 217 us: layer(): up = jnp.dot(a, w['w_up'], preferred_element_type=jnp.float32)]
    reduce_scatter x6 -> x0, waiting for transfers between devices: 271 us -> none  [step(): lax.psum_scatter(by_w[name], 'dp', scatter_dimension=0, tiled=True)]
    all_gather x6 -> x0, waiting for transfers between devices: 185 us -> none  [fetched(): lax.all_gather(w[number], 'dp', axis=0, tiled=True)]
    psum x1 -> x0, blocking collectives: 22.6 us -> none  [step(): squares = lax.psum(sum((jnp.sum(g * g) for g in gradients)), 'dp')]
    unnamed x26 -> x6, local copies, waits for them, and re-layouts: 21.2 us -> 1.17 us
    reduce_sum x4 -> x1, other arithmetic: 16.8 us -> 1.29 us  [step(): factor = jnp.minimum(1.0, 0.5 * lax.rsqrt(jnp.sum(squares) / count + 1e-30))]
  transfers between devices with their start and end apart: 12 -> 0, of which waited for: 10 -> 0; matrix products, arithmetic and copies ran while one was open for 40% -> 0% of each run, Pallas kernels for 0% -> 0%
where the time goes in v1:
time: 735 us; the launch traced here: 727 us
  Pallas kernels  685 us (93%)
  other arithmetic  38.8 us (5%)
    pallas_call x1, Pallas kernels, gradients_of(): pl.pallas_call(kernel, out_shape=outs, in_specs=[anywhere] * 5, out_specs...  685 us
    convert_element_type x2, other arithmetic, adamw(): return ((w - 0.02 * step).astype(BF), m, v)  37.5 us

profile of v1, /device:TPU:0, one launch (start us, length us, event | category | flops | bytes accessed | tf_op | source)
XLA Modules:
  0.0 726.7 jit_solution(2750235537388209649)
XLA Ops:
  0.6 684.9 %step.1 = (bf16[2,192,4224]{2,1,0:T(8,128)(2,1)}, bf16[2,192,4224]{2,1,0:T(8,128)(2,1)}, bf16[2,528,1536]{2,1,0:T(8,128)(2,1)}, f32[8,128]{1,0:T(8,128)}, bf16[2...) custom-call(bf16[2048,1536]{1,0:T(8,128)(2,1)} %bitcast.2, ...), custom_call_target="tpu_custom_call" | custom-call | tf_op jit(solution)/shard_map/step/pallas_call | solution.py:638
  685.6 1.3 reduce_sum.9
  687.6 0.0 copy-start
  687.6 0.0 copy-start.1
  687.6 0.0 copy-start.2
  687.6 14.0 %fusion.8 = (bf16[2,528,1536]{2,1,0:T(8,128)(2,1)}, f32[2,528,1536]{2,1,0:T(8,128)}, f32[2,528,1536]{2,1,0:T(8,128)}) fusion(bf16[2,528,1536]{2,1,0:T(8,128)(2,1)} %wd.1, f32[]{:T(128)S(6)} %min_shard_map.3, bf16[2,528,1536]{2,1,0:T(8,128)(2,1)} %get-tuple-element.16, f32[2,528,1536]{2,1,0:T(8,128)} %param.21, f32[2,528,1536]{2,1,0:T(8,128)} %param.18), kind=kLoop, calls=%fused_computation.17 | loop fusion | flops 27574272 | bytes 35684356 | tf_op jit(solution)/shard_map/convert_element_type | solution.py:653
  701.6 0.0 copy-done
  701.6 0.0 copy-done.1
  701.6 1.2 copy-done.2
  702.8 23.5 %fusion.2 = (bf16[2,192,4224]{2,1,0:T(8,128)(2,1)}, f32[2,192,4224]{2,1,0:T(8,128)}, f32[2,192,4224]{2,1,0:T(8,128)}, bf16[2,192,4224]{2,1,0:T(8,128)(2,1)}, f32...) fusion(bf16[2,192,4224]{2,1,0:T(8,128)(2,1)S(1)} %copy-done, f32[]{:T(128)S(6)} %min_shard_map.3, ...), kind=kLoop, calls=%fused_computation.11 | loop fusion | flops 55148544 | bytes 71368704 | tf_op jit(solution)/shard_map/convert_element_type | solution.py:653
Async XLA Ops:
  687.6 14.0 %copy-start = (bf16[2,192,4224]{2,1,0:T(8,128)(2,1)S(1)}, bf16[2,192,4224]{2,1,0:T(8,128)(2,1)}, u32[]{:S(2)}) copy-start(bf16[2,192,4224]{2,1,0:T(8,128)(2,1)} %wg.1) | copy-start | bytes 9732100
  687.6 14.0 %copy-start.1 = (bf16[2,192,4224]{2,1,0:T(8,128)(2,1)S(1)}, bf16[2,192,4224]{2,1,0:T(8,128)(2,1)}, u32[]{:S(2)}) copy-start(bf16[2,192,4224]{2,1,0:T(8,128)(2,1)} %wu.1) | copy-start | bytes 9732100
  687.6 15.2 %copy-start.2 = (bf16[2,192,4224]{2,1,0:T(8,128)(2,1)S(1)}, bf16[2,192,4224]{2,1,0:T(8,128)(2,1)}, u32[]{:S(2)}) copy-start(bf16[2,192,4224]{2,1,0:T(8,128)(2,1)} %get-tuple-element.13) | copy-start | bytes 9732100

commit v2 on v1

--- a/solution.py
+++ b/solution.py
@@ -14,10 +14,11 @@
 TALL, HALF, MAIN = 1024, 768, 4096
 NC = MAIN // COL
 RDC, ND, PER = 176, 9, 26
-Q, RING = 2 * PER, 12
+Q, RING = 2 * PER, 13
 DOWN, BOTH, TAIL = (RDC, WIDE), (RG, WIDE), (RG, COL)
 OX, OY, OS, FX, FY, SX, SY, SD = range(8)
-UNITS = ((0, (0, 8)), (0, (8, NC)), (0, None), (1, (0, 8)), (1, (8, 12)), (1, (12, NC)), (1, None))
+PARTS = ((0, 8), (8, 12), (12, NC), None)
+NP = len(PARTS)
 YES, NO = True, False
 S2, S3, S4 = 2, 3, 4
 PAIR = (0, 1)
@@ -28,7 +29,7 @@
 
 
 def block(i, n):
-    return pl.ds(pl.multiple_of(i, 8), n)
+    return pl.ds(i, n) if isinstance(i, int) else pl.ds(pl.multiple_of(i, 8), n)
 
 
 def start(copies):
@@ -63,7 +64,7 @@
     return up * (s + silu * (1.0 - s)), silu, (silu * up).astype(BF)
 
 
-def kernel(x, dy, wg, wu, wd, gg, gu, gd, squares, WG, WU, WD, aT, hT, R, Rt, h1, own, inx, iny, DG, DU,
+def kernel(x, dy, wg, wu, wd, gg, gu, gd, squares, WGU, WD, aT, hT, R, Rt, h1, own, inx, iny, DGU,
            A, Y, dgi, d2r, sq, send, recv, keeps, dgi_sem, in_sem, out_sem, d2r_sem, d2s_sem, own_sem, sq_send, sq_recv, ld, ldl, st, credit, room):
     me = lax.axis_index("dp")
     core, y_, x_ = me % S2, (me // 2) % S2, me // 4
@@ -88,8 +89,8 @@
     whose = (me, me, me, yn, xn, xn, yn, dg)
 
     def half(u, p, dev):
-        l, blocks = UNITS[u]
-        refs = (wg, wu, wd) if dev is None else (WG, WU, WD)
+        l, blocks = u[0], PARTS[u[1]]
+        refs = (wg, wu, wd) if dev is None else (WGU.at[0], WGU.at[1], WD)
         ref, height, rows, top, cols = refs[2], RD, RD // 2, p * (RD // 2), pl.ds(0, D)
         if blocks:
             lo, hi = blocks[0] * COL, FF if blocks[1] == NC else blocks[1] * COL
@@ -100,10 +101,11 @@
 
     def hop(u, k, p):
         src = half(u, p, None if k <= OS else whose[k])
-        return remote(src, half(u, p, whose[k]), send.at[u, k, p], recv.at[u, k, p], to_whom[k])
+        i = u[0] * NP + u[1]
+        return remote(src, half(u, p, whose[k]), send.at[i, k, p], recv.at[i, k, p], to_whom[k])
 
     def keep(u):
-        return [local(half(u, p, None), half(u, p, me), keeps.at[u, p]) for p in PAIR]
+        return [local(half(u, p, None), half(u, p, me), keeps.at[u[0] * NP + u[1], p]) for p in PAIR]
 
     def first(u):
         start(hop(u, k, p) for k, p in ((OX, 0), (OY, 1), (OX, 1), (OY, 0), (OS, 0), (OS, 1)))
@@ -115,8 +117,11 @@
     def point1(u):
         arrived(u, (OX, 0), (OY, 1))
         start([hop(u, FY, 0), hop(u, FX, 1)])
-        if u + 1 < len(UNITS):
-            first(u + 1)
+        l, i = u
+        if i + 1 < NP:
+            first((l, i + 1))
+        else:
+            when(l < 1, lambda: first((l + 1, 0)))
         start([hop(u, SX, 0), hop(u, SY, 1)])
 
     def point2(u):
@@ -159,13 +164,11 @@
 
             wait(put_T(l, c, aT) for c in (n - 2, n - 1))
 
-        def gate_up(u, points, Wb, r32):
-            l, (lo, end) = UNITS[u]
-            n = end - lo
-            hi = end == NC
+        def gate_up(l, Wb, r32):
+            due = ((1, point1, 1), (3, point2, 1), (5, point3, 1), (8, point1, 2), (10, point2, 2), (11, point3, 2), (14, point1, 3))
 
             def get(j):
-                return [local(W.at[l, :, cut(j, COL)], Wb.at[j % S3, :, cut(i, COL)], ld.at[j % S3, i]) for i, W in enumerate((WG, WU))]
+                return [local(WGU.at[i, l, :, cut(j, COL)], Wb.at[j % S3, :, cut(i, COL)], ld.at[j % S3, i]) for i in PAIR]
 
             def put(j):
                 return [local(r32.at[j % S2], R.at[l, j], st.at[j % S2, 1]), put_T(l, j, hT)]
@@ -178,45 +181,39 @@
                     by_gate, by_up, hid = gated(r[:, :w], r[:, w:])
                     r32[out, rows, pl.ds(0, w)] = by_gate
                     r32[out, rows, pl.ds(w, w)] = by_up
-                    if l == 0:
-                        H[rows, pl.ds(MAIN, w) if w == LAST else cut(j, COL)] = hid
+                    H[rows, pl.ds(MAIN, w) if w == LAST else cut(j, COL)] = hid
                     hTs[out, pl.ds(0, w), rows] = hid.T
 
-            ws = [local(W.at[l, :, pl.ds(MAIN, LAST)], Wb.at[NC % S3, :, cut(i, LAST)], ld.at[NC % S3, i]) for i, W in enumerate((WG, WU))]
-            start(get(lo) + get(lo + 1))
-
-            @pl.loop(lo, lo + n)
+            ws = [local(WGU.at[i, l, :, pl.ds(MAIN, LAST)], Wb.at[NC % S3, :, cut(i, LAST)], ld.at[NC % S3, i]) for i in PAIR]
+            def begin(part):
+                if part:
+                    point4((l, part))
+                lo = PARTS[part][0]
+                start(get(lo) + get(lo + 1))
+
+            begin(0)
+
+            @pl.loop(0, NC)
             def _(j):
+                for part in (1, 2):
+                    pl.when(j == PARTS[part][0])(lambda: begin(part))
                 wait(get(j))
-                pl.when(j + 2 < lo + n)(lambda: start(get(j + 2)))
-                pl.when(j >= lo + 2)(lambda: wait(put(j - 2)))
+                in_part = j + 2 < NC
+                for _, lo in (PARTS[0], PARTS[1]):
+                    in_part = jnp.logical_and(in_part, jnp.logical_and(j + 2 != lo, j + 1 != lo))
+                pl.when(in_part)(lambda: start(get(j + 2)))
+                pl.when(j == NC - 2)(lambda: start(ws))
+                pl.when(j >= 2)(lambda: wait(put(j - 2)))
                 work(j, COL, j % S3, j % S2)
                 start(put(j))
-                if hi:
-                    pl.when(j == NC - 2)(lambda: start(ws))
-                for i, (do, unit) in points:
-                    pl.when(j == lo + i)(lambda: do(unit))
-
-            wait(put(lo + n - 2))
-            if hi:
-                wait(ws)
-                work(NC, LAST, NC % S3, 0)
-                outs = [local(r32.at[0, :, pl.ds(0, COL)], Rt.at[l], st.at[0, 1]), local(hTs.at[0, pl.ds(0, LAST)], hT.at[l, pl.ds(MAIN, LAST), :], st.at[0, 0])]
-                start(outs)
-                wait(outs)
-            wait(put(lo + n - 1))
-
-        def both(units, *points):
-            def body(Wb, r32):
-                for u, due in zip(units, points):
-                    gate_up(u, due, Wb, r32)
-                    if u < units[-1]:
-                        late = [do for _, (do, unit) in due if unit == u + 1]
-                        for do in (point1, point2, point3, point4):
-                            if do not in late:
-                                do(u + 1)
-
-            pl.run_scoped(body, pltpu.VMEM((S3, D, WIDE), BF), pltpu.VMEM((S2, T, WIDE), F32))
+                for i, point, part in due:
+                    pl.when(j == i)(lambda: point((l, part)))
+
+            wait(put(NC - 2) + ws)
+            work(NC, LAST, NC % S3, 0)
+            outs = [local(r32.at[0, :, pl.ds(0, COL)], Rt.at[l], st.at[0, 1]), local(hTs.at[0, pl.ds(0, LAST)], hT.at[l, pl.ds(MAIN, LAST), :], st.at[0, 0])]
+            start(outs)
+            wait(outs + put(NC - 1))
 
         def down(Wd, xs):
             n = D // COL
@@ -237,30 +234,33 @@
                     r = dot(H[rows, :], Wd[c % S2]).astype(BF)
                     A[rows, cut(c, COL)] = (xs[c % S2, rows, :].astype(F32) + r.astype(F32)).astype(BF)
 
-                pl.when(c == 3)(lambda: point1(3))
+                pl.when(c == 3)(lambda: point1((1, 0)))
 
         load = local(x, A, ld.at[0, 0])
         load.start()
         load.wait()
-        norm()
-        transposed(0)
-        point1(0)
-        rest(0)
-        both((0, 1), [(5, (point1, 1))], [(5, (point1, 2))])
-        rest(2)
-        pl.run_scoped(down, pltpu.VMEM((S2, FF, COL), BF), pltpu.VMEM((S2, T, COL), BF))
-        save = local(A, h1, ld.at[0, 0])
-        save.start()
-        save.wait()
-        norm()
-        transposed(1)
-        rest(3)
-        both((3, 4, 5), [(1, (point1, 4)), (3, (point2, 4)), (5, (point3, 4))], [(0, (point1, 5)), (2, (point2, 5))], [(2, (point1, 6))])
-
-    first(0)
+
+        @pl.loop(0, 2)
+        def _(l):
+            norm()
+            transposed(l)
+            pl.when(l == 0)(lambda: point1((0, 0)))
+            rest((l, 0))
+            pl.run_scoped(functools.partial(gate_up, l), pltpu.VMEM((S3, D, WIDE), BF), pltpu.VMEM((S2, T, WIDE), F32))
+
+            @pl.when(l == 0)
+            def _():
+                rest((0, NP - 1))
+                pl.run_scoped(down, pltpu.VMEM((S2, FF, COL), BF), pltpu.VMEM((S2, T, COL), BF))
+                save = local(A, h1, ld.at[0, 0])
+                save.start()
+                save.wait()
+
+    first((0, 0))
     by_y = local(dy, Y, st.at[3, 0])
     by_y.start()
-    for u in range(len(UNITS)):
+    units = [(l, i) for l in PAIR for i in range(NP)]
+    for u in units:
         start(keep(u))
     pl.run_scoped(forward, pltpu.VMEM((T, FF), BF), pltpu.VMEM((S2, COL, T), BF))
 
@@ -384,11 +384,8 @@
                 @pl.loop(2, ND)
                 def _(c):
                     one(c, YES, YES)
-                    if l == 1:
-                        pl.when(c == 2)(lambda: point2(6))
-                        pl.when(c == 7)(lambda: point3(6))
-                    else:
-                        serve_some(c - 5, S4, base, S3, DOWN)
+                    pl.when(jnp.logical_and(c == 2, l == 1))(lambda: point2((1, NP - 1)))
+                    pl.when(jnp.logical_and(c == 7, l == 1))(lambda: point3((1, NP - 1)))
 
                 then()
 
@@ -401,148 +398,141 @@
         def layer_gradients(base, l):
             g = base + ND
 
-            def outer(Wd, Rb, dgu):
+            def outer(Rb):
                 lhs = lambda L: [local(aT.at[l, block(dev * RG, RG), :], L.at[cut(b, RG), :], ldl.at[2, b]) for b, dev in enumerate(order)]
                 is_last = lambda c: isinstance(c, int) and c == NC
                 kind = lambda c: TAIL if is_last(c) else BOTH
-                part = lambda c: dgu[c % S4, :, pl.ds(0, kind(c)[1])]
+                part = lambda dgu, c: dgu[c % S4, :, pl.ds(0, kind(c)[1])]
 
                 def get(c):
                     k = c % S2
                     if is_last(c):
-                        return [local(WD.at[l, pl.ds(MAIN, LAST), :], Wd.at[k, pl.ds(0, LAST), :], ld.at[k, 0]), local(Rt.at[l], Rb.at[k, :, pl.ds(0, COL)], ld.at[k, 1])]
-                    return [local(WD.at[l, cut(c, COL), :], Wd.at[k], ld.at[k, 0]), local(R.at[l, c], Rb.at[k], ld.at[k, 1])]
-
-                def put(c):
+                        return [local(WD.at[l, pl.ds(MAIN, LAST), :], A.at[block(k * COL, LAST), :], ld.at[k, 0]), local(Rt.at[l], Rb.at[k, :, pl.ds(0, COL)], ld.at[k, 1])]
+                    return [local(WD.at[l, cut(c, COL), :], A.at[cut(k, COL), :], ld.at[k, 0]), local(R.at[l, c], Rb.at[k], ld.at[k, 1])]
+
+                def put(c, dgu):
                     w, cols = (LAST, pl.ds(MAIN, LAST)) if is_last(c) else (COL, cut(c, COL))
-                    return [local(dgu.at[c % S4, :, cut(i, w)], W.at[:, cols], st.at[c % S4, i]) for i, W in enumerate((DG, DU))]
-
-                def step(s, L, do_f, do_s, do_m):
+                    return [local(dgu.at[c % S4, :, cut(i, w)], DGU.at[i, :, cols], st.at[c % S4, i]) for i in PAIR]
+
+                def step(s, L, dgu, do_f, do_s, do_m):
                     c, e = s - 1, s - 3
                     if do_f:
                         wait(get(s))
                         when(jnp.logical_and(s > 0, s < NC - 1) if not isinstance(s, int) else 0 < s < NC - 1, lambda: start(get(s + 1)))
-                        if l == 1:
-                            when(s >= 4, lambda: wait(put(s - 4)))
+                        when(s >= 4, lambda: wait(put(s - 4, dgu)))
                     if do_m:
                         before_add(g + e, kind(e))
-                        sums(g + e, kind(e), L, part(e))
+                        sums(g + e, kind(e), L, part(dgu, e))
                     if do_s:
-                        theirs(g + c, kind(c), L, part(c))
+                        theirs(g + c, kind(c), L, part(dgu, c))
                     if do_f:
                         w = LAST if is_last(s) else COL
-                        d = dot(Y[...], Wd[s % S2, pl.ds(0, w), :], nt=YES).astype(BF).astype(F32)
+                        d = dot(Y[...], A[block(s % S2 * COL, w), :], nt=YES).astype(BF).astype(F32)
                         for i in PAIR:
                             dgu[s % S4, :, cut(i, w)] = (d * Rb[s % S2, :, cut(i, w)]).astype(BF)
                     if do_s:
                         send_d2d(g + c, kind(c))
-                    if do_f and l == 1:
-                        start(put(s))
+                    if do_f:
+                        start(put(s, dgu))
                     if do_m:
                         after_add(g + e, kind(e))
 
                 def down_served(s):
-                    if l == 1:
-                        serve_some(2 * s, 12, base, ND, DOWN)
-                        serve_some(2 * s + 1, 12, base, ND, DOWN)
-                    else:
-                        serve_some(s, ND - S3, base + S3, ND - S3, DOWN)
+                    serve_some(2 * s, 12, base, ND, DOWN)
+                    serve_some(2 * s + 1, 12, base, ND, DOWN)
 
                 def ahead():
-                    if l == 1:
-                        point4(6)
+                    pl.when(l == 1)(lambda: point4((1, NP - 1)))
                     start(get(0) + get(1))
 
-                def body(L):
+                def body(L, dgu):
                     start(lhs(L))
-                    step(0, L, YES, NO, NO)
+                    step(0, L, dgu, YES, NO, NO)
                     down_served(jnp.int32(0))
                     wait(lhs(L))
 
                     @pl.loop(1, 3)
                     def _(s):
-                        step(s, L, YES, YES, NO)
+                        step(s, L, dgu, YES, YES, NO)
                         down_served(s)
 
                     @pl.loop(3, NC)
                     def _(s):
-                        step(s, L, YES, YES, YES)
+                        step(s, L, dgu, YES, YES, YES)
                         pl.when(s == NC - 2)(lambda: start(get(NC)))
                         down_served(s)
-                        serve_some(s - 6, 11, g, 10, BOTH)
-
-                    step(NC, L, YES, YES, YES)
-                    serve(g + 9, BOTH)
-                    step(NC + 1, L, NO, YES, YES)
-                    step(NC + 2, L, NO, NO, YES)
-                    step(NC + 3, L, NO, NO, YES)
-                    if l == 1:
-                        for c in range(NC - 3, NC + 1):
-                            wait(put(c))
+                        serve_some(s - 8, 8, g, 8, BOTH)
+
+                    step(NC, L, dgu, YES, YES, YES)
+                    serve(g + 8, BOTH)
+                    step(NC + 1, L, dgu, NO, YES, YES)
+                    step(NC + 2, L, dgu, NO, NO, YES)
+                    step(NC + 3, L, dgu, NO, NO, YES)
+                    for c in range(NC - 3, NC + 1):
+                        wait(put(c, dgu))
 
                 down_gradient(base, l, ahead)
-                pl.run_scoped(body, pltpu.VMEM((D, T), BF))
-
-            V = pltpu.VMEM
-            pl.run_scoped(outer, V((S2, COL, D), BF), V((S2, T, WIDE), F32), V((S4, T, WIDE), BF))
+                pl.run_scoped(body, pltpu.VMEM((D, T), BF), pltpu.VMEM((S4, T, WIDE), BF))
+
+            pl.run_scoped(outer, pltpu.VMEM((S2, T, WIDE), F32))
 
         def input_gradient():
             m, n = T // WIDE, D // HALF
             steps = m * n
 
             def body(W, X, hb):
-                def get_x(i, src):
-                    return [local(src.at[cut(i % m * 4 + k, LAST), :], X.at[i % S2, cut(k, LAST), :], ldl.at[i % S2, k]) for k in range(4)]
-
-                def get_w(k, src):
-                    return local(src.at[1, cut(k % n, HALF), :], W.at[k % S2], ld.at[k % S2, 1])
-
-                get_w(0, WG).start()
-                start(get_x(0, DG))
-                for up, (grad, weight) in enumerate(((DG, WG), (DU, WU))):
-                    @pl.loop(0, steps)
-                    def _(i):
-                        k = n * up + i // m
-
-                        @pl.when(i % m == 0)
-                        def _():
-                            get_w(k, weight).wait()
-                            pl.when(i < steps - m)(lambda: get_w(k + 1, weight).start())
-                            if not up:
-                                pl.when(i == steps - m)(lambda: get_w(n, WU).start())
-
-                        wait(get_x(i, grad))
-                        pl.when(i < steps - 1)(lambda: start(get_x(i + 1, grad)))
-                        if not up:
-                            pl.when(i == steps - 1)(lambda: start(get_x(0, DU)))
-                        r = dot(X[i % S2], W[k % S2], nt=YES).astype(BF)
-                        place = (cut(i % m, WIDE), cut(i // m, HALF))
-                        A[place] = (A[place].astype(F32) + r.astype(F32)).astype(BF) if up else r
-                        serve_some(steps * up + i, 11, ND + 10, 6, BOTH)
-
-                get_h = lambda i: local(h1.at[cut(i, COL), :], hb.at[i % S2], st.at[i % S2, 0])
-                get_h(0).start()
+                def get_x(i):
+                    src = DGU.at[i // steps]
+                    return [local(src.at[cut(i % m * S4 + k, LAST), :], X.at[i % S2, cut(k, LAST), :], ldl.at[i % S2, k]) for k in range(S4)]
+
+                def get_w(k):
+                    return local(WGU.at[k // n, 1, cut(k % n, HALF), :], W.at[k % S2], ld.at[k % S2, 1])
+
+                get_h = lambda i: local(h1.at[cut(i, LAST), :], hb.at[i % S4], st.at[i % S4, 0])
+                start(get_h(i) for i in range(S4))
+                get_w(0).start()
+                start(get_x(0))
+
+                @pl.loop(0, 2 * steps)
+                def _(i):
+                    k = i // m
+
+                    @pl.when(i % m == 0)
+                    def _():
+                        get_w(k).wait()
+                        pl.when(k < 2 * n - 1)(lambda: get_w(k + 1).start())
+
+                    wait(get_x(i))
+                    pl.when(i < 2 * steps - 1)(lambda: start(get_x(i + 1)))
+                    r = dot(X[i % S2], W[k % S2], nt=YES).astype(BF)
+                    place = (cut(i % m, WIDE), cut(k % n, HALF))
+                    before = jnp.where(i < steps, 0.0, A[place].astype(F32))
+                    A[place] = (before + r.astype(F32)).astype(BF)
+                    serve_some(i, 13, ND + 9, 7, BOTH)
+
                 serve(PER - 1, TAIL)
 
-                @pl.loop(0, T // COL)
+                @pl.loop(0, T // LAST)
                 def _(i):
                     get_h(i).wait()
-                    pl.when(i < T // COL - 1)(lambda: get_h(i + 1).start())
-                    rows = cut(i, COL)
-                    f, b = hb[i % S2].astype(F32), A[rows, :].astype(F32)
+                    rows = cut(i, LAST)
+                    f, b = hb[i % S4].astype(F32), A[rows, :].astype(F32)
                     ms = jnp.mean(f * f, -1, keepdims=YES) + 1e-6
                     scale = lax.rsqrt(ms)
                     c = jnp.sum(f * b, -1, keepdims=YES) * (-0.5 * (scale / ms)) * (1.0 / D)
                     back = (b * scale + c * (2.0 * f)).astype(BF)
                     Y[rows, :] = (Y[rows, :].astype(F32) + back.astype(F32)).astype(BF)
+                    pl.when(i + S4 < T // LAST)(lambda: get_h(i + S4).start())
 
             V = pltpu.VMEM
-            pl.run_scoped(body, V((S2, HALF, FF), BF), V((S2, WIDE, FF), BF), V((S2, COL, D), BF))
+            pl.run_scoped(body, V((S2, HALF, FF), BF), V((S2, WIDE, FF), BF), V((S4, LAST, D), BF))
 
         by_y.wait()
-        layer_gradients(0, 1)
-        input_gradient()
-        layer_gradients(PER, 0)
+
+        @pl.loop(0, 2)
+        def _(i):
+            layer_gradients(i * PER, 1 - i)
+            pl.when(i == 0)(input_gradient)
 
         for q in (Q - 2, Q - 1):
             by_kind(jnp.int32(q), wait_own)
@@ -581,8 +571,8 @@
                 by_kind(q, lambda q, kind: start(put(q, kind)))
 
             acc[...] = jnp.zeros_like(acc)
-            n = 7
-            left = Q - n
+            n = 6
+            left = Q - 8
             fetch(jnp.int32(0))
             fetch(jnp.int32(1))
 
@@ -607,7 +597,7 @@
         def _(q):
             by_kind(q, release)
 
-        for u in range(len(UNITS)):
+        for u in units:
             for k in range(8):
                 for p in ((1,) if k == FX else (0,) if k == FY else (0, 1)):
                     hop(u, k, p).wait_send()
@@ -630,10 +620,10 @@
         [(8, LAST)],
     ]
     outs = [S(s, BF) for s in narrow] + [S(s, F32) for s in wide]
-    outs += [S((S2, D, FF), BF), S((S2, D, FF), BF), S((S2, FF, D), BF), S((S2, D, T), BF), S((S2, FF, T), BF), S((S2, NC, T, WIDE), F32), S((S2, T, COL), F32), S((T, D), BF)]
-    outs += [S((Q, RG, WIDE), F32), S((Q, RG, WIDE), BF), S((Q, RG, WIDE), BF), S((T, FF), BF), S((T, FF), BF)]
+    outs += [S((2, 2, D, FF), BF), S((S2, FF, D), BF), S((S2, D, T), BF), S((S2, FF, T), BF), S((S2, NC, T, WIDE), F32), S((S2, T, COL), F32), S((T, D), BF)]
+    outs += [S((Q, RG, WIDE), F32), S((Q, RG, WIDE), BF), S((Q, RG, WIDE), BF), S((2, T, FF), BF)]
     scratch = [V((T, D), BF), V((T, D), BF), V((RING, 2, RG, COL), BF), V((S3, 4 * RG, WIDE), BF), V((8, 8, LAST), F32)]
-    scratch += [dma((len(UNITS), 8, 2)), dma((len(UNITS), 8, 2)), dma((len(UNITS), 2)), dma((RING, 2)), dma((Q, 4)), dma((RING, 6)), dma((3,)), dma((2,)), dma((2,)), dma((7,)), dma((7,))]
+    scratch += [dma((2 * NP, 8, 2)), dma((2 * NP, 8, 2)), dma((2 * NP, 2)), dma((RING, 2)), dma((Q, 4)), dma((RING, 6)), dma((3,)), dma((2,)), dma((2,)), dma((7,)), dma((7,))]
     scratch += [dma((3, 2)), dma((3, 8)), dma((4, 2)), regular, regular((2,))]
     return pl.pallas_call(
         kernel,
@@ -646,21 +636,43 @@
     )(x, dy, wg, wu, wd)[:4]
 
 
-def adamw(w, m, v, g):
-    m = 0.9 * m + 0.1 * g
-    v = 0.95 * v + 0.05 * g * g
-    step = m * lax.rsqrt(v + 1e-8) + 0.1 * w
-    return (w - 0.02 * step).astype(BF), m, v
+STEPS = 4
+
+
+def adamw_kernel(count, squares, *refs):
+    factor = jnp.minimum(1.0, 0.5 * lax.rsqrt(jnp.sum(squares[...], keepdims=YES) / count + 1e-30))
+    g, w, m, v, new_w, new_m, new_v = (refs[i : i + 3] for i in range(0, len(refs), 3))
+    for i in range(3):
+        by = g[i][...].astype(F32) * factor
+        first = 0.9 * m[i][...] + 0.1 * by
+        second = 0.95 * v[i][...] + 0.05 * by * by
+        old = w[i][...].astype(F32)
+        new_w[i][...] = (old - 0.02 * (first * lax.rsqrt(second + 1e-8) + 0.1 * old)).astype(BF)
+        new_m[i][...] = first
+        new_v[i][...] = second
+
+
+def adamw(gradients, squares, count, weights, m, v):
+    flat = [a.reshape(-1, a.shape[-1]) for a in (*gradients, *weights, *m, *v)]
+    spec = lambda a: pl.BlockSpec((a.shape[0] // STEPS, a.shape[1]), lambda i: (i, 0))
+    outs = [jax.ShapeDtypeStruct(a.shape, a.dtype) for a in flat[3:]]
+    new = pl.pallas_call(
+        functools.partial(adamw_kernel, count),
+        grid=(STEPS,),
+        out_shape=outs,
+        in_specs=[pl.BlockSpec(squares.shape, lambda i: (0, 0))] + [spec(a) for a in flat],
+        out_specs=[spec(a) for a in outs],
+        compiler_params=pltpu.CompilerParams(vmem_limit_bytes=66_000_000),
+        name="adamw",
+    )(squares, *flat)
+    return tuple(a.reshape(2, -1, a.shape[-1]) for a in new)
 
 
 def solution(mesh):
     def step(x, dy, *arrays):
         weights, m, v = (arrays[i : i + 3] for i in (0, 3, 6))
         *gradients, squares = gradients_of(x[0], dy[0], *weights)
-        count = mesh.shape["dp"] * sum(g.size for g in gradients)
-        factor = jnp.minimum(1.0, 0.5 * lax.rsqrt(jnp.sum(squares) / count + 1e-30))
-        new = [adamw(w.astype(F32), m, v, g.astype(F32) * factor) for w, m, v, g in zip(weights, m, v, gradients, strict=YES)]
-        return tuple(one[which] for which in range(3) for one in new)
+        return adamw(gradients, squares, mesh.shape["dp"] * sum(g.size for g in gradients), weights, m, v)
 
     states, cuts = P(("rep", "dp"), None, None), P(None, "dp", None)
     return jax.shard_map(

time: 735 us -> 714 us (0.971); the launches traced: 727 us -> 714 us
  other arithmetic: 38.8 us -> 0 us
  Pallas kernels: 685 us -> 713 us
    convert_element_type x2 -> x0, other arithmetic: 37.5 us -> none  [adamw(): return ((w - 0.02 * step).astype(BF), m, v)]
    pallas_call x0 -> x1, Pallas kernels: none -> 35.7 us  [adamw(): pl.pallas_call(functools.partial(adamw_kernel, count), grid=(STEPS,), out...]
    pallas_call x1, Pallas kernels: 685 us -> 677 us  [gradients_of(): pl.pallas_call(kernel, out_shape=outs, in_specs=[anywhere] * 5, out_specs...]
where the time goes in v2:
time: 714 us
  Pallas kernels  713 us (100%)
    pallas_call x1, Pallas kernels, gradients_of(): pl.pallas_call(kernel, out_shape=outs, in_specs=[anywhere] * 5, out_specs...  677 us
    pallas_call x1, Pallas kernels, adamw(): pl.pallas_call(functools.partial(adamw_kernel, count), grid=(STEPS,), out...  35.7 us

profile of v2, /device:TPU:0, one launch (start us, length us, event | category | flops | bytes accessed | tf_op | source)
XLA Modules:
  0.0 713.8 jit_solution(8675832544882771848)
XLA Ops:
  0.6 677.3 %step.1 = (bf16[2,192,4224]{2,1,0:T(8,128)(2,1)}, bf16[2,192,4224]{2,1,0:T(8,128)(2,1)}, bf16[2,528,1536]{2,1,0:T(8,128)(2,1)}, f32[8,128]{1,0:T(8,128)}, bf16[2...) custom-call(bf16[2048,1536]{1,0:T(8,128)(2,1)} %bitcast.32, ...), custom_call_target="tpu_custom_call" | custom-call | tf_op jit(solution)/shard_map/step/pallas_call | solution.py:628
  678.0 35.7 %adamw.1 = (bf16[384,4224]{1,0:T(8,128)(2,1)}, bf16[384,4224]{1,0:T(8,128)(2,1)}, bf16[1056,1536]{1,0:T(8,128)(2,1)}, f32[384,4224]{1,0:T(8,128)}, f32[384,4224]...) custom-call(f32[8,128]{1,0:T(8,128)} %get-tuple-element.22.squares, ...), custom_call_target="tpu_custom_call" | custom-call | tf_op jit(solution)/shard_map/adamw/pallas_call | solution.py:659

commit v3 on v2

--- a/solution.py
+++ b/solution.py
@@ -17,7 +17,7 @@
 Q, RING = 2 * PER, 13
 DOWN, BOTH, TAIL = (RDC, WIDE), (RG, WIDE), (RG, COL)
 OX, OY, OS, FX, FY, SX, SY, SD = range(8)
-PARTS = ((0, 8), (8, 12), (12, NC), None)
+PARTS = ((0, 5), (5, 9), (9, 13), (13, NC), None)
 NP = len(PARTS)
 YES, NO = True, False
 S2, S3, S4 = 2, 3, 4
@@ -165,7 +165,8 @@
             wait(put_T(l, c, aT) for c in (n - 2, n - 1))
 
         def gate_up(l, Wb, r32):
-            due = ((1, point1, 1), (3, point2, 1), (5, point3, 1), (8, point1, 2), (10, point2, 2), (11, point3, 2), (14, point1, 3))
+            due = ((0, point2, 1), (2, point3, 1), (4, point1, 2), (6, point2, 2), (8, point3, 2), (9, point1, 3), (11, point2, 3), (12, point3, 3))
+            due += ((NC - 1, point1, 4),)
 
             def get(j):
                 return [local(WGU.at[i, l, :, cut(j, COL)], Wb.at[j % S3, :, cut(i, COL)], ld.at[j % S3, i]) for i in PAIR]
@@ -186,8 +187,7 @@
 
             ws = [local(WGU.at[i, l, :, pl.ds(MAIN, LAST)], Wb.at[NC % S3, :, cut(i, LAST)], ld.at[NC % S3, i]) for i in PAIR]
             def begin(part):
-                if part:
-                    point4((l, part))
+                point4((l, part))
                 lo = PARTS[part][0]
                 start(get(lo) + get(lo + 1))
 
@@ -195,11 +195,11 @@
 
             @pl.loop(0, NC)
             def _(j):
-                for part in (1, 2):
+                for part in range(1, NP - 1):
                     pl.when(j == PARTS[part][0])(lambda: begin(part))
                 wait(get(j))
                 in_part = j + 2 < NC
-                for _, lo in (PARTS[0], PARTS[1]):
+                for lo, _ in PARTS[1 : NP - 1]:
                     in_part = jnp.logical_and(in_part, jnp.logical_and(j + 2 != lo, j + 1 != lo))
                 pl.when(in_part)(lambda: start(get(j + 2)))
                 pl.when(j == NC - 2)(lambda: start(ws))
@@ -234,7 +234,7 @@
                     r = dot(H[rows, :], Wd[c % S2]).astype(BF)
                     A[rows, cut(c, COL)] = (xs[c % S2, rows, :].astype(F32) + r.astype(F32)).astype(BF)
 
-                pl.when(c == 3)(lambda: point1((1, 0)))
+                pl.when(c == 0)(lambda: point1((1, 0)))
 
         load = local(x, A, ld.at[0, 0])
         load.start()
@@ -244,14 +244,22 @@
         def _(l):
             norm()
             transposed(l)
-            pl.when(l == 0)(lambda: point1((0, 0)))
-            rest((l, 0))
+
+            @pl.when(l == 0)
+            def _():
+                point1((0, 0))
+                point2((0, 0))
+                point3((0, 0))
+
+            point1((l, 1))
             pl.run_scoped(functools.partial(gate_up, l), pltpu.VMEM((S3, D, WIDE), BF), pltpu.VMEM((S2, T, WIDE), F32))
 
             @pl.when(l == 0)
             def _():
                 rest((0, NP - 1))
                 pl.run_scoped(down, pltpu.VMEM((S2, FF, COL), BF), pltpu.VMEM((S2, T, COL), BF))
+                point2((1, 0))
+                point3((1, 0))
                 save = local(A, h1, ld.at[0, 0])
                 save.start()
                 save.wait()
@@ -384,9 +392,9 @@
                 @pl.loop(2, ND)
                 def _(c):
                     one(c, YES, YES)
-                    pl.when(jnp.logical_and(c == 2, l == 1))(lambda: point2((1, NP - 1)))
-                    pl.when(jnp.logical_and(c == 7, l == 1))(lambda: point3((1, NP - 1)))
-
+                    pl.when(jnp.logical_and(c == 4, l == 1))(lambda: point2((1, NP - 1)))
+
+                pl.when(l == 1)(lambda: point3((1, NP - 1)))
                 then()
 
                 @pl.loop(ND, ND + 2)
@@ -417,7 +425,8 @@
                 def step(s, L, dgu, do_f, do_s, do_m):
                     c, e = s - 1, s - 3
                     if do_f:
-                        wait(get(s))
+                        if do_s:
+                            wait(get(s))
                         when(jnp.logical_and(s > 0, s < NC - 1) if not isinstance(s, int) else 0 < s < NC - 1, lambda: start(get(s + 1)))
                         when(s >= 4, lambda: wait(put(s - 4, dgu)))
                     if do_m:
@@ -442,11 +451,14 @@
                     serve_some(2 * s + 1, 12, base, ND, DOWN)
 
                 def ahead():
+                    start(get(c)[1] for c in PAIR)
+
+                def body(L, dgu):
                     pl.when(l == 1)(lambda: point4((1, NP - 1)))
-                    start(get(0) + get(1))
-
-                def body(L, dgu):
+                    get(0)[0].start()
+                    wait(get(0))
                     start(lhs(L))
+                    get(1)[0].start()
                     step(0, L, dgu, YES, NO, NO)
                     down_served(jnp.int32(0))
                     wait(lhs(L))
@@ -585,14 +597,15 @@
             def _(q):
                 one(q)
 
+            sq[...] = sum(acc[:, cut(i, LAST)] for i in range(WIDE // LAST))
+            start(tell)
             for q in (Q - 2, Q - 1):
                 by_kind(jnp.int32(q), lambda q, kind: wait(put(q, kind)))
-            sq[me] = sum(acc[:, cut(i, LAST)] for i in range(WIDE // LAST))
-
+
+        tell = [local(sq, squares.at[me], ld.at[0, 0])]
+        tell += [remote(sq, squares.at[me], sq_send.at[k], sq_recv.at[k], dev) for k, dev in enumerate(everyone)]
         V = pltpu.VMEM
         pl.run_scoped(finish, V((S3, RG, WIDE), F32), V((S3, 2, RG, WIDE), BF), V((S2, RG, WIDE), BF), V((8, WIDE), F32))
-        tell = [remote(sq.at[me], sq.at[me], sq_send.at[k], sq_recv.at[k], dev) for k, dev in enumerate(everyone)]
-        start(tell)
         @pl.loop(Q - RING, Q)
         def _(q):
             by_kind(q, release)
@@ -602,10 +615,6 @@
                 for p in ((1,) if k == FX else (0,) if k == FY else (0, 1)):
                     hop(u, k, p).wait_send()
         wait(tell)
-        sq[0] = sum(sq[i] for i in range(8))
-        out = local(sq.at[0], squares, ld.at[0, 0])
-        out.start()
-        out.wait()
 
     V = pltpu.VMEM
     pl.run_scoped(backward, V((RING, 3, RG, WIDE), BF), V((RING, 2, RG, COL), F32), V((S2, 4 * RG, WIDE), BF), V((S2, RG, WIDE), F32))
@@ -617,12 +626,12 @@
     anywhere = pl.BlockSpec(memory_space=pl.ANY)
     narrow, wide = [
         [(2, RG, FF), (2, RG, FF), (2, RD, D)],
-        [(8, LAST)],
+        [(8, 8, LAST)],
     ]
     outs = [S(s, BF) for s in narrow] + [S(s, F32) for s in wide]
     outs += [S((2, 2, D, FF), BF), S((S2, FF, D), BF), S((S2, D, T), BF), S((S2, FF, T), BF), S((S2, NC, T, WIDE), F32), S((S2, T, COL), F32), S((T, D), BF)]
     outs += [S((Q, RG, WIDE), F32), S((Q, RG, WIDE), BF), S((Q, RG, WIDE), BF), S((2, T, FF), BF)]
-    scratch = [V((T, D), BF), V((T, D), BF), V((RING, 2, RG, COL), BF), V((S3, 4 * RG, WIDE), BF), V((8, 8, LAST), F32)]
+    scratch = [V((T, D), BF), V((T, D), BF), V((RING, 2, RG, COL), BF), V((S3, 4 * RG, WIDE), BF), V((8, LAST), F32)]
     scratch += [dma((2 * NP, 8, 2)), dma((2 * NP, 8, 2)), dma((2 * NP, 2)), dma((RING, 2)), dma((Q, 4)), dma((RING, 6)), dma((3,)), dma((2,)), dma((2,)), dma((7,)), dma((7,))]
     scratch += [dma((3, 2)), dma((3, 8)), dma((4, 2)), regular, regular((2,))]
     return pl.pallas_call(
@@ -640,7 +649,7 @@
 
 
 def adamw_kernel(count, squares, *refs):
-    factor = jnp.minimum(1.0, 0.5 * lax.rsqrt(jnp.sum(squares[...], keepdims=YES) / count + 1e-30))
+    factor = jnp.minimum(1.0, 0.5 * lax.rsqrt(jnp.sum(jnp.sum(squares[...], 0), keepdims=YES) / count + 1e-30))
     g, w, m, v, new_w, new_m, new_v = (refs[i : i + 3] for i in range(0, len(refs), 3))
     for i in range(3):
         by = g[i][...].astype(F32) * factor
@@ -660,7 +669,7 @@
         functools.partial(adamw_kernel, count),
         grid=(STEPS,),
         out_shape=outs,
-        in_specs=[pl.BlockSpec(squares.shape, lambda i: (0, 0))] + [spec(a) for a in flat],
+        in_specs=[pl.BlockSpec(squares.shape, lambda i: (0, 0, 0))] + [spec(a) for a in flat],
         out_specs=[spec(a) for a in outs],
         compiler_params=pltpu.CompilerParams(vmem_limit_bytes=66_000_000),
         name="adamw",

time: 714 us -> 712 us (level)
  no operation moved by 1% of the time
where the time goes in v3:
time: 712 us; the launch traced here: 711 us
  Pallas kernels  710 us (100%)
    pallas_call x1, Pallas kernels, gradients_of(): pl.pallas_call(kernel, out_shape=outs, in_specs=[anywhere] * 5, out_specs...  674 us
    pallas_call x1, Pallas kernels, adamw(): pl.pallas_call(functools.partial(adamw_kernel, count), grid=(STEPS,), out...  35.6 us

profile of v3, /device:TPU:0, one launch (start us, length us, event | category | flops | bytes accessed | tf_op | source)
XLA Modules:
  0.0 710.7 jit_solution(6543078552630934625)
XLA Ops:
  0.6 674.3 %step.1 = (bf16[2,192,4224]{2,1,0:T(8,128)(2,1)}, bf16[2,192,4224]{2,1,0:T(8,128)(2,1)}, bf16[2,528,1536]{2,1,0:T(8,128)(2,1)}, f32[8,8,128]{2,1,0:T(8,128)}, bf...) custom-call(bf16[2048,1536]{1,0:T(8,128)(2,1)} %bitcast.32, ...), custom_call_target="tpu_custom_call" | custom-call | tf_op jit(solution)/shard_map/step/pallas_call | solution.py:637
  674.9 35.6 %adamw.1 = (bf16[384,4224]{1,0:T(8,128)(2,1)}, bf16[384,4224]{1,0:T(8,128)(2,1)}, bf16[1056,1536]{1,0:T(8,128)(2,1)}, f32[384,4224]{1,0:T(8,128)}, f32[384,4224]...) custom-call(f32[8,8,128]{2,1,0:T(8,128)} %get-tuple-element.22.squares, ...), custom_call_target="tpu_custom_call" | custom-call | tf_op jit(solution)/shard_map/adamw/pallas_call | solution.py:668

commit v4 on v3

--- a/solution.py
+++ b/solution.py
@@ -366,7 +366,7 @@
             pl.when(jnp.logical_and(b > a, jnp.logical_and(i >= 0, i < steps)))(lambda: serve(lo + a, kind))
 
         def down_gradient(base, l, then):
-            def body(L):
+            def body(L, hb):
                 def get(t):
                     return [local(hT.at[l, block(dev * RD + t * RDC, RDC), :], L.at[t % S2, cut(b, RDC), :], ldl.at[t % S2, b]) for b, dev in enumerate(order)]
 
@@ -384,7 +384,26 @@
                     if do_m:
                         after_add(q - 2, DOWN)
 
+                get_h = lambda i: local(h1.at[cut(i, LAST), :], hb.at[i % S4], st.at[i % S4, 0])
+
+                def back_through_norm():
+                    start(get_h(i) for i in range(S4))
+
+                    @pl.loop(0, T // LAST)
+                    def _(i):
+                        get_h(i).wait()
+                        rows = cut(i, LAST)
+                        f, b = hb[i % S4].astype(F32), A[rows, :].astype(F32)
+                        ms = jnp.mean(f * f, -1, keepdims=YES) + 1e-6
+                        scale = lax.rsqrt(ms)
+                        c = jnp.sum(f * b, -1, keepdims=YES) * (scale / ms) * (-1.0 / D)
+                        back = (b * scale + c * f).astype(BF)
+                        Y[rows, :] = (Y[rows, :].astype(F32) + back.astype(F32)).astype(BF)
+                        pl.when(i + S4 < T // LAST)(lambda: get_h(i + S4).start())
+
                 start(get(0))
+                pl.when(l == 0)(back_through_norm)
+
                 @pl.loop(0, 2)
                 def _(c):
                     one(c, YES, NO)
@@ -401,7 +420,7 @@
                 def _(c):
                     one(c, NO, YES)
 
-            pl.run_scoped(body, pltpu.VMEM((S2, 8 * RDC, T), BF))
+            pl.run_scoped(body, pltpu.VMEM((S2, 8 * RDC, T), BF), pltpu.VMEM((S4, LAST, D), BF))
 
         def layer_gradients(base, l):
             g = base + ND
@@ -455,10 +474,9 @@
 
                 def body(L, dgu):
                     pl.when(l == 1)(lambda: point4((1, NP - 1)))
-                    get(0)[0].start()
+                    start(get(c)[0] for c in PAIR)
                     wait(get(0))
                     start(lhs(L))
-                    get(1)[0].start()
                     step(0, L, dgu, YES, NO, NO)
                     down_served(jnp.int32(0))
                     wait(lhs(L))
@@ -473,10 +491,10 @@
                         step(s, L, dgu, YES, YES, YES)
                         pl.when(s == NC - 2)(lambda: start(get(NC)))
                         down_served(s)
-                        serve_some(s - 8, 8, g, 8, BOTH)
+                        serve_some(s - 8 - l, 8, g, 8, BOTH)
 
                     step(NC, L, dgu, YES, YES, YES)
-                    serve(g + 8, BOTH)
+                    serve(g + 8 - l, BOTH)
                     step(NC + 1, L, dgu, NO, YES, YES)
                     step(NC + 2, L, dgu, NO, NO, YES)
                     step(NC + 3, L, dgu, NO, NO, YES)
@@ -492,7 +510,7 @@
             m, n = T // WIDE, D // HALF
             steps = m * n
 
-            def body(W, X, hb):
+            def body(W, X):
                 def get_x(i):
                     src = DGU.at[i // steps]
                     return [local(src.at[cut(i % m * S4 + k, LAST), :], X.at[i % S2, cut(k, LAST), :], ldl.at[i % S2, k]) for k in range(S4)]
@@ -500,8 +518,6 @@
                 def get_w(k):
                     return local(WGU.at[k // n, 1, cut(k % n, HALF), :], W.at[k % S2], ld.at[k % S2, 1])
 
-                get_h = lambda i: local(h1.at[cut(i, LAST), :], hb.at[i % S4], st.at[i % S4, 0])
-                start(get_h(i) for i in range(S4))
                 get_w(0).start()
                 start(get_x(0))
 
@@ -520,24 +536,11 @@
                     place = (cut(i % m, WIDE), cut(k % n, HALF))
                     before = jnp.where(i < steps, 0.0, A[place].astype(F32))
                     A[place] = (before + r.astype(F32)).astype(BF)
-                    serve_some(i, 13, ND + 9, 7, BOTH)
+                    serve_some(i, 14, ND + 8, 8, BOTH)
 
                 serve(PER - 1, TAIL)
 
-                @pl.loop(0, T // LAST)
-                def _(i):
-                    get_h(i).wait()
-                    rows = cut(i, LAST)
-                    f, b = hb[i % S4].astype(F32), A[rows, :].astype(F32)
-                    ms = jnp.mean(f * f, -1, keepdims=YES) + 1e-6
-                    scale = lax.rsqrt(ms)
-                    c = jnp.sum(f * b, -1, keepdims=YES) * (-0.5 * (scale / ms)) * (1.0 / D)
-                    back = (b * scale + c * (2.0 * f)).astype(BF)
-                    Y[rows, :] = (Y[rows, :].astype(F32) + back.astype(F32)).astype(BF)
-                    pl.when(i + S4 < T // LAST)(lambda: get_h(i + S4).start())
-
-            V = pltpu.VMEM
-            pl.run_scoped(body, V((S2, HALF, FF), BF), V((S2, WIDE, FF), BF), V((S4, LAST, D), BF))
+            pl.run_scoped(body, pltpu.VMEM((S2, HALF, FF), BF), pltpu.VMEM((S2, WIDE, FF), BF))
 
         by_y.wait()
 

time: 712 us -> 710 us (level)
  no operation moved by 1% of the time
where the time goes in v4:
time: 710 us; the launch traced here: 709 us
  Pallas kernels  709 us (100%)
    pallas_call x1, Pallas kernels, gradients_of(): pl.pallas_call(kernel, out_shape=outs, in_specs=[anywhere] * 5, out_specs...  673 us
    pallas_call x1, Pallas kernels, adamw(): pl.pallas_call(functools.partial(adamw_kernel, count), grid=(STEPS,), out...  35.6 us

profile of v4, /device:TPU:0, one launch (start us, length us, event | category | flops | bytes accessed | tf_op | source)
XLA Modules:
  0.0 709.5 jit_solution(16447883005238832199)
XLA Ops:
  0.6 673.0 %step.1 = (bf16[2,192,4224]{2,1,0:T(8,128)(2,1)}, bf16[2,192,4224]{2,1,0:T(8,128)(2,1)}, bf16[2,528,1536]{2,1,0:T(8,128)(2,1)}, f32[8,8,128]{2,1,0:T(8,128)}, bf...) custom-call(bf16[2048,1536]{1,0:T(8,128)(2,1)} %bitcast.32, ...), custom_call_target="tpu_custom_call" | custom-call | tf_op jit(solution)/shard_map/step/pallas_call | solution.py:640
  673.7 35.6 %adamw.1 = (bf16[384,4224]{1,0:T(8,128)(2,1)}, bf16[384,4224]{1,0:T(8,128)(2,1)}, bf16[1056,1536]{1,0:T(8,128)(2,1)}, f32[384,4224]{1,0:T(8,128)}, f32[384,4224]...) custom-call(f32[8,8,128]{2,1,0:T(8,128)} %get-tuple-element.22.squares, ...), custom_call_target="tpu_custom_call" | custom-call | tf_op jit(solution)/shard_map/adamw/pallas_call | solution.py:671
